TPU v7x, 32 devices: a whole 2x2x4 slice. The times are simulated.
32 devices in a mesh: groups: 2 (over y), seq: 4 (over z), blk: 2 (over x), cfg: 2 (over core).
Axes of the slice: x: 2, y: 2, z: 4, core: 2. Of those that a mesh axis runs over, the one named last changes fastest.
Arguments:
- queries: bfloat16 [4, 320, 4096], P(('groups', 'cfg'), ('seq', 'blk')), parts along dimension 0, may hold values from -6 to 6
- keys: bfloat16 [4, 320, 4096], P(('groups', 'cfg'), ('seq', 'blk')), parts along dimension 0, may hold values from -6 to 6
- values: bfloat16 [4, 320, 4096], P(('groups', 'cfg'), ('seq', 'blk')), parts along dimension 0, may hold values from -6 to 6
- ref_keys: bfloat16 [4, 1024, 4096], P(('groups', 'cfg'), 'seq'), parts along dimension 0, may hold values from -6 to 6
- ref_values: bfloat16 [4, 1024, 4096], P(('groups', 'cfg'), 'seq'), parts along dimension 0, may hold values from -6 to 6
- ref_len: int32 [4], P(('groups', 'cfg')), parts along dimension 0, may hold values from 256 to 1024, as said below
- step_index: int32 [2], P('groups'), parts along dimension 0, may hold values from 0 to 49
- guide: float32 [2], P('groups'), parts along dimension 0, may hold values from 3 to 6
- latent: float32 [320, 128], P(('groups', 'seq', 'blk', 'cfg')), parts along dimension 0, may hold values from -6 to 6
- w_out: bfloat16 [4096, 64], replicated, may hold values from -1 to 1
Outputs:
- latent_next: float32 [320, 128], P(('groups', 'seq', 'blk', 'cfg')), parts along dimension 0
- denoised: float32 [320, 128], P(('groups', 'seq', 'blk', 'cfg')), parts along dimension 0
There are 2 independent parts, one for each index of `groups`. A program takes and returns all parts, laid end to end along the dimension named above; an argument that names none is the same for every part. Nothing has to cross between parts.
Inputs may be any that keep to these rules, and one draw needn't show every extreme that they name: `ref_len`: one of the two branches has exactly 1024 valid reference tokens.
All inputs are finite; a program needn't handle non-finite values.
Results may differ from a plain program's by a relative error of at most 0.005.
Values may be sent and summed in bfloat16 or wider, within the bound.
No kernel may reach another device: no remote copies, remote signals or barrier semaphores. Data moves between devices by JAX's collectives and lax.ppermute only.
A program may use at most 128 MiB of HBM per device.

v0:
```python
from functools import partial

import jax
import jax.numpy as jnp
from jax import lax
from jax.experimental import pallas as pl
from jax.experimental.pallas import tpu as pltpu
from jax.sharding import PartitionSpec as P

HD = 128
STEPS = 50
LOG2E = 1.4426950408889634
NEG = -1e30
SCALE = HD ** (-0.5) * LOG2E

SMEM = pl.BlockSpec(memory_space=pltpu.SMEM)
VMEM = pl.BlockSpec(memory_space=pltpu.VMEM)


def in_vmem(array):
    return pltpu.with_memory_space_constraint(array, pltpu.VMEM)


def in_hbm(array):
    return pltpu.with_memory_space_constraint(array, pltpu.HBM)


def dot_t(left, right):
    return lax.dot_general(
        left, right, (((1,), (1,)), ((), ())), preferred_element_type=jnp.float32
    )


def exchange(value, axis, pairs):
    return lax.ppermute(value, axis, pairs)


def swap(value, axis, mask):
    return exchange(value, axis, [(i, i ^ mask) for i in range(lax.axis_size(axis))])


def head_columns(head):
    return slice(head * HD, (head + 1) * HD)


def head_scores(query, keys, refkeys, bias, some):
    scores = {}
    for h in some:
        columns = head_columns(h)
        scores[h, 0] = dot_t(query[:, columns], keys[:, columns])
        scores[h, 1] = dot_t(query[:, columns], refkeys[:, columns]) + bias
    return scores


def head_exps(scores):
    tops = {item: jnp.max(score, axis=1, keepdims=True) for item, score in scores.items()}
    exps = {item: jnp.exp2((score - tops[item]) * SCALE) for item, score in scores.items()}
    totals = {item: jnp.sum(exps[item], axis=1, keepdims=True) for item in scores}
    return tops, exps, totals


def place_columns(target, lane, columns):
    for (h, which), column in columns.items():
        target = jnp.where(lane == which * 32 + h, column, target)
    return target


def head_outputs(exps, values, refvalues, some):
    return {
        h: jnp.concatenate(
            [
                jnp.dot(
                    exps[h, which], value[:, head_columns(h)], preferred_element_type=jnp.float32
                ).astype(jnp.bfloat16)
                for which, value in ((0, values), (1, refvalues))
            ],
            axis=1,
        )
        for h in some
    }


def fill_rows(scratch, refs):
    start = 0
    for ref in refs:
        scratch[start : start + ref.shape[0], :] = ref[...]
        start += ref.shape[0]


def fill_weight(weight, w_ref, heads):
    weight[...] = jnp.zeros_like(weight)
    out = w_ref.shape[0]
    for h in range(heads):
        weight[:out, 2 * h * HD : (2 * h + 1) * HD] = w_ref[:, head_columns(h)]
        weight[out:, (2 * h + 1) * HD : 2 * (h + 1) * HD] = w_ref[:, head_columns(h)]


def is_inner():
    place = lax.axis_index("seq")
    return jnp.logical_or(place == 1, place == 2)


def is_inner():
    place = lax.axis_index("seq")
    return jnp.logical_or(place == 1, place == 2)


def sigma_of(index):
    frac = 1.0 - index.astype(jnp.float32) / STEPS
    return 5.0 * frac / (1.0 + 4.0 * frac)


def load_kernel(heads, ref_len, step_index, guide, *refs):
    sources, w_ref, bias, scalars, targets, weight, w_here, sems = (
        refs[:5], refs[5], refs[6], refs[7], refs[8:13], refs[13], refs[14], refs[15]
    )
    copies = [
        pltpu.make_async_copy(source, target, sems.at[i])
        for i, (source, target) in enumerate(zip((w_ref, *sources), (w_here, *targets)))
    ]
    for copy in copies:
        copy.start()
    valid = ref_len[0] - lax.axis_index("seq") * sources[3].shape[0]
    index = lax.broadcasted_iota(jnp.int32, bias.shape, 1)
    bias[...] = jnp.where(index < valid, 0.0, jnp.float32(NEG))
    sig_now = sigma_of(step_index[0])
    factor = jnp.where(lax.axis_index("cfg") == 0, guide[0], 1.0 - guide[0])
    for i, scalar in enumerate((factor, sig_now, sigma_of(step_index[0] + 1) - sig_now)):
        scalars[8 * i : 8 * i + 8, :] = jnp.full((8, 128), scalar, jnp.float32)
    copies[0].wait()
    fill_weight(weight, w_here, heads)
    for copy in copies[1:]:
        copy.wait()


def score_rows(heads, query, keys, refk, bias, exps_out):
    rows = query.shape[0]
    count, others = refk.shape[0], keys.shape[0]
    span = count + 128
    lane = lax.broadcasted_iota(jnp.int32, (rows, 128), 1)
    top_columns = jnp.zeros((rows, 128), jnp.float32)
    sum_columns = jnp.ones((rows, 128), jnp.float32)
    for first in range(0, heads, 8):
        some = range(first, first + 8)
        tops, exps, totals = head_exps(head_scores(query, keys, refk, bias[0:1], some))
        for h in some:
            start = h * span
            exps_out[:, start : start + count] = exps[h, 1].astype(jnp.bfloat16)
            start += count
            exps_out[:, start : start + others] = exps[h, 0].astype(jnp.bfloat16)
        top_columns = place_columns(top_columns, lane, tops)
        sum_columns = place_columns(sum_columns, lane, totals)
    top_columns = top_columns * SCALE
    return top_columns + jnp.log2(sum_columns), top_columns


def value_rows(heads, exps, values, refv, weight, out):
    count, others = refv.shape[0], values.shape[0]
    span = count + 128
    for first in range(0, heads, 16):
        some = range(first, first + 16)
        parts = {}
        for h in some:
            start = h * span
            parts[h, 1] = exps[:, start : start + count]
            parts[h, 0] = exps[:, start + count : start + count + others]
        outputs = head_outputs(parts, values, refv, some)
        for h in some:
            out[head_columns(h), :] = dot_t(weight[:, 2 * h * HD : 2 * (h + 1) * HD], outputs[h])


def early_scores_kernel(heads, own, near, k0, k1, refk, bias, exps, lse, top, keys, query):
    fill_rows(query, (own, near))
    fill_rows(keys, (k0, k1))
    lse[...], top[...] = score_rows(heads, query, keys, refk, bias, exps)


def early_values_kernel(heads, exps, v0, v1, refv, weight, out, values):
    fill_rows(values, (v0, v1))
    value_rows(heads, exps, values, refv, weight, out)


def late_scores_kernel(
    heads, mid_in, mid_out, far_in, far_out, keys, refk, bias, lse_early, top_early,
    exps, lse, top, query,
):
    @pl.when(is_inner())
    def _():
        fill_rows(query, (mid_in, far_in))

    @pl.when(jnp.logical_not(is_inner()))
    def _():
        fill_rows(query, (mid_out, far_out))

    low = lax.broadcasted_iota(jnp.int32, lse.shape, 1) < 64
    late = score_rows(heads, query, keys, refk, bias, exps)
    for out, early, mine in ((lse, lse_early, late[0]), (top, top_early, late[1])):
        out[...] = jnp.where(low, early[...], pltpu.roll(mine, 64, 1))


def late_values_kernel(heads, exps, values, refv, weight, out):
    value_rows(heads, exps, values, refv, weight, out)


def combine_kernel(
    heads, scalars, own, o1, o2, o3, top, early, late, b0, b1, b2, b3, velocity
):
    rows = own.shape[0]
    count = rows // 2
    everyone = [own[...]]
    for mask, ref in ((1, o1), (2, o2), (3, o3)):
        value = ref[...]
        if mask & 1:
            value = jnp.concatenate([value[count:], value[:count]], axis=0)
        if mask & 2:
            value = pltpu.roll(value, 64, 1)
        everyone.append(value)
    share = share_of(top[...], everyone) * scalars[0:1, :]
    turned = jnp.transpose(share)
    sums = []
    for base, parts in ((0, early), (64, late)):
        total = [None, None]
        for h in range(heads):
            for which in range(2):
                start = h * HD + which * 64
                row = base + which * 32 + h
                value = parts[start : start + 64, :] * turned[row : row + 1, :]
                total[h % 2] = value if total[h % 2] is None else total[h % 2] + value
        sums.append(total[0] + total[1])
    velocity[...] = jnp.transpose(jnp.concatenate(sums, axis=0))
    even = velocity[pl.ds(0, count, stride=2), :]
    odd = velocity[pl.ds(1, count, stride=2), :]
    low = lax.broadcasted_iota(jnp.int32, even.shape, 1) < 64
    first = jnp.where(low, even, pltpu.roll(odd, 64, 1))
    second = jnp.where(low, pltpu.roll(even, 64, 1), odd)
    half = count // 2
    b0[...], b1[...], b2[...], b3[...] = first[:half], first[half:], second[:half], second[half:]


def share_of(own, everyone):
    top = everyone[0]
    for value in everyone[1:]:
        top = jnp.maximum(top, value)
    total = jnp.exp2(everyone[0] - top)
    for value in everyone[1:]:
        total = total + jnp.exp2(value - top)
    return jnp.exp2(own - top) * (1.0 / total)


def split_kernel(b0, r1, r2, r3, kept, given):
    total = (b0[...] + r1[...]) + (r2[...] + r3[...])
    half = total.shape[0] // 2
    first = lax.axis_index("cfg") == 0
    kept[...] = jnp.where(first, total[:half], total[half:])
    given[...] = jnp.where(first, total[half:], total[:half])


def euler_kernel(scalars, latent, kept, taken, latent_next, denoised):
    guided = kept[...] + taken[...]
    latent_next[...] = latent[...] + scalars[16:17, :] * guided
    denoised[...] = latent[...] - scalars[8:9, :] * guided


def call(kernel, arrays, outs, scratch=(), mib=12, flops=0):
    return pl.pallas_call(
        kernel,
        in_specs=[VMEM] * len(arrays),
        out_specs=[VMEM] * len(outs),
        out_shape=outs,
        scratch_shapes=list(scratch),
        compiler_params=pltpu.CompilerParams(vmem_limit_bytes=mib << 20),
        cost_estimate=pl.CostEstimate(flops=flops, bytes_accessed=0, transcendentals=0),
    )(*[in_vmem(a) for a in arrays])


def line_of_four(
    query, keys, values, refk, refv, ref_len, step_index, guide, latent, w_t
):
    count, width = query.shape
    heads = width // HD
    rows, others = 2 * count, refk.shape[0]
    f32, bf16 = jnp.float32, jnp.bfloat16
    sources = (query, keys, values, refk, refv)
    k_other = swap(keys, "blk", 1)
    v_other = swap(values, "blk", 1)
    far_in = exchange(query, "seq", [(1, 2), (2, 1)])
    near = swap(query, "seq", 1)
    far_out = exchange(query, "seq", [(0, 3), (3, 0)])
    mid_in = exchange(query, "seq", [(0, 2), (3, 1)])
    mid_out = exchange(far_in, "seq", [(2, 3), (1, 0)])
    bias, scalars, query, keys, values, refk, refv, weight = pl.pallas_call(
        partial(load_kernel, heads),
        in_specs=[SMEM] * 3 + [pl.BlockSpec(memory_space=pltpu.HBM)] * 6,
        out_specs=[VMEM] * 8,
        out_shape=[pltpu.VMEM((8, others), f32), pltpu.VMEM((24, 128), f32)]
        + [pltpu.VMEM(a.shape, a.dtype) for a in sources]
        + [pltpu.VMEM((128, 2 * width), bf16)],
        scratch_shapes=[pltpu.VMEM(w_t.shape, w_t.dtype), pltpu.SemaphoreType.DMA((6,))],
        compiler_params=pltpu.CompilerParams(vmem_limit_bytes=2 << 20),
        cost_estimate=pl.CostEstimate(
            flops=10000000, bytes_accessed=4 * refk.size, transcendentals=0
        ),
        name="load",
    )(ref_len, step_index, guide, *[in_hbm(a) for a in (*sources, w_t)])
    exps_shape = pltpu.VMEM((rows, heads * (others + 128)), bf16)
    columns = pltpu.VMEM((rows, 128), f32)
    stacked = pltpu.VMEM((rows, width), bf16)
    partial_shape = pltpu.VMEM((width, rows), f32)
    flops = 2 * rows * (others + rows) * width
    exps_e, lse_e, top_e, keys = call(
        partial(early_scores_kernel, heads),
        (query, near, keys, k_other, refk, bias),
        [exps_shape, columns, columns, stacked], [stacked], flops=flops,
    )
    early, values = call(
        partial(early_values_kernel, heads),
        (exps_e, values, v_other, refv, weight), [partial_shape, stacked], flops=flops,
    )
    exps_l, lse, top = call(
        partial(late_scores_kernel, heads),
        (mid_in, mid_out, far_in, far_out, keys, refk, bias, lse_e, top_e),
        [exps_shape, columns, columns], [stacked], flops=flops,
    )
    o3 = swap(lse, "seq", 3)
    o2 = swap(lse, "seq", 2)
    o1 = swap(lse, "seq", 1)
    (late,) = call(
        partial(late_values_kernel, heads),
        (exps_l, values, refv, weight), [partial_shape], flops=flops,
    )
    block = pltpu.VMEM((count // 2, 128), f32)
    blocks = call(
        partial(combine_kernel, heads),
        (scalars, lse, o1, o2, o3, top, early, late), [block] * 4, [columns],
    )
    r3 = swap(blocks[3], "seq", 3)
    r2 = swap(blocks[2], "seq", 2)
    r1 = swap(blocks[1], "seq", 1)
    half = pltpu.VMEM(latent.shape, latent.dtype)
    kept, given = call(split_kernel, (blocks[0], r1, r2, r3), [half] * 2, mib=2)
    taken = swap(given, "cfg", 1)
    result = jax.ShapeDtypeStruct(latent.shape, latent.dtype)
    return call(euler_kernel, (scalars, latent, kept, taken), [result] * 2, mib=2)


def attend_kernel(heads, valid, query, keys, values, refk, refv, w_ref, out, lse, share, weight):
    step = pl.program_id(0)
    fill_weight(weight, w_ref, heads)
    index = lax.broadcasted_iota(jnp.int32, (1, refk.shape[0]), 1)
    bias = jnp.where(index < valid[0], 0.0, jnp.float32(NEG))
    lane = lax.broadcasted_iota(jnp.int32, lse.shape, 1)

    @pl.when(step == 0)
    def _():
        lse[...] = jnp.zeros_like(lse)
        share[...] = jnp.zeros_like(share)

    for h in range(heads):
        tops, exps, totals = head_exps(head_scores(query, keys, refk, bias, (h,)))
        exps = {item: value.astype(jnp.bfloat16) for item, value in exps.items()}
        outputs = head_outputs(exps, values, refv, (h,))
        out[:, head_columns(h)] = dot_t(outputs[h], weight[:, 2 * h * HD : 2 * (h + 1) * HD])
        for which in range(2):
            here = lane == which * 32 + step * heads + h
            top = tops[h, which] * SCALE
            share[...] = jnp.where(here, top, share[...])
            lse[...] = jnp.where(here, top + jnp.log2(totals[h, which]), lse[...])


def combine_any_kernel(heads, factor, top, everyone, parts, out, pairs):
    share = share_of(top[...], [everyone[i] for i in range(everyone.shape[0])])
    rows = share.shape[0]
    low = lax.broadcasted_iota(jnp.int32, (rows, 128), 1) < 64
    even = lax.broadcasted_iota(jnp.int32, (rows, 128), 0) % 2 == 0
    total = jnp.zeros((rows, 128), jnp.float32)
    for h in range(heads):
        both = jnp.where(low, share[:, h : h + 1], share[:, 32 + h : 33 + h])
        total += parts[:, head_columns(h)] * both
    total = total + pltpu.roll(total, 64, 1)
    pairs[...] = jnp.where(even == low, total * factor[0], 0.0)
    rows = out.shape[0]
    out[...] = pairs[pl.ds(0, rows, stride=2), :] + pairs[pl.ds(1, rows, stride=2), :]


def any_line(
    query, keys, values, refk, refv, ref_len, step_index, guide, latent, w_t
):
    line = lax.axis_size("seq")
    valid = ref_len - lax.axis_index("seq") * refk.shape[0]
    branch = lax.axis_index("cfg")
    factor = jnp.where(branch == 0, guide, 1.0 - guide)
    query = lax.all_gather(query, "seq", axis=0, tiled=True)
    keys = lax.all_gather(keys, "blk", axis=0, tiled=True)
    values = lax.all_gather(values, "blk", axis=0, tiled=True)
    rows, width = query.shape
    heads = width // HD
    some = 4
    columns = some * HD
    arrays = (query, keys, values, refk, refv, w_t)
    out, lse, top = pl.pallas_call(
        partial(attend_kernel, some),
        grid=(heads // some,),
        in_specs=[SMEM]
        + [pl.BlockSpec((a.shape[0], columns), lambda i: (0, i)) for a in arrays],
        out_specs=[
            pl.BlockSpec((rows, columns), lambda i: (0, i)),
            pl.BlockSpec((rows, 128), lambda i: (0, 0)),
            pl.BlockSpec((rows, 128), lambda i: (0, 0)),
        ],
        out_shape=[
            jax.ShapeDtypeStruct((rows, width), jnp.float32),
            jax.ShapeDtypeStruct((rows, 128), jnp.float32),
            jax.ShapeDtypeStruct((rows, 128), jnp.float32),
        ],
        scratch_shapes=[pltpu.VMEM((128, 2 * columns), jnp.bfloat16)],
        compiler_params=pltpu.CompilerParams(dimension_semantics=("arbitrary",)),
        name="attend",
    )(valid, *arrays)
    everyone = lax.all_gather(lse, "seq", axis=0, tiled=False)
    velocity = pl.pallas_call(
        partial(combine_any_kernel, heads),
        in_specs=[SMEM] + [VMEM] * 3,
        out_specs=VMEM,
        out_shape=jax.ShapeDtypeStruct((rows // 2, 128), jnp.float32),
        scratch_shapes=[pltpu.VMEM((rows, 128), jnp.float32)],
        name="combine",
    )(factor, top, everyone, out)
    blocks = velocity.reshape(line, -1, 128)
    mine = lax.all_to_all(blocks, "seq", split_axis=0, concat_axis=0, tiled=True).sum(0)
    half_rows = mine.shape[0] // 2
    kept = lax.dynamic_slice_in_dim(mine, branch * half_rows, half_rows, 0)
    given = lax.dynamic_slice_in_dim(mine, (1 - branch) * half_rows, half_rows, 0)
    guided = kept + swap(given, "cfg", 1)
    sig_now = sigma_of(step_index[0])
    sig_next = sigma_of(step_index[0] + 1)
    return (latent + (sig_next - sig_now) * guided, latent - sig_now * guided)


def on_device(
    queries, keys, values, ref_keys, ref_values, ref_len, step_index, guide, latent, w_out
):
    special = lax.axis_size("seq") == 4 and lax.axis_size("blk") == 2
    return tuple(
        (line_of_four if special else any_line)(
            queries[0], keys[0], values[0], ref_keys[0], ref_values[0],
            ref_len, step_index, guide, latent, w_out.T,
        )
    )


def solution(mesh):
    in_specs = (
        P(("groups", "cfg"), ("seq", "blk"), None),
        P(("groups", "cfg"), ("seq", "blk"), None),
        P(("groups", "cfg"), ("seq", "blk"), None),
        P(("groups", "cfg"), "seq", None),
        P(("groups", "cfg"), "seq", None),
        P(("groups", "cfg")),
        P("groups"),
        P("groups"),
        P(("groups", "seq", "blk", "cfg"), None),
        P(),
    )
    out_specs = (P(("groups", "seq", "blk", "cfg"), None), P(("groups", "seq", "blk", "cfg"), None))
    return jax.shard_map(
        on_device, mesh=mesh, in_specs=in_specs, out_specs=out_specs, check_vma=False
    )
```

profile of v0, /device:TPU:1, one launch (start us, length us, event | category | flops | bytes accessed | tf_op | source)
XLA Modules:
  0.0 52.9 jit_solution(6668422585940754865)
XLA Ops:
  0.6 0.7 %collective-permute-start.1 = (bf16[40,4096]{1,0:T(8,128)(2,1)}, bf16[40,4096]{1,0:T(8,128)(2,1)S(1)}, u32[]{:S(2)}, u32[]{:S(2)}) collective-permute-start(bf16[40,4096]{1,0:T(8,128)(2,1)} %bitcast.11), channel_id=1, source_target_pairs={{4,8},{8,4},{5,9},{9,5},{6,10},{10,6},{7,11},{11,7},{20,24},{24,20... | collective-permute-start | bytes 983048 | tf_op jit(solution)/shard_map/ppermute | solution.py:35
  1.3 4.7 %collective-permute-start.4 = (bf16[40,4096]{1,0:T(8,128)(2,1)}, bf16[40,4096]{1,0:T(8,128)(2,1)S(1)}, u32[]{:S(2)}, u32[]{:S(2)}) collective-permute-start(bf16[40,4096]{1,0:T(8,128)(2,1)} %bitcast.12), channel_id=1, source_target_pairs={{0,4},{4,0},{8,12},{12,8},{1,5},{5,1},{9,13},{13,9},{2,6},{6,2},{1... | collective-permute-start | bytes 983048 | tf_op jit(solution)/shard_map/ppermute | solution.py:35
  6.0 1.2 %collective-permute-start.5 = (bf16[40,4096]{1,0:T(8,128)(2,1)}, bf16[40,4096]{1,0:T(8,128)(2,1)S(1)}, u32[]{:S(2)}, u32[]{:S(2)}) collective-permute-start(bf16[40,4096]{1,0:T(8,128)(2,1)} %bitcast.9), channel_id=1, source_target_pairs={{0,2},{2,0},{1,3},{3,1},{4,6},{6,4},{5,7},{7,5},{8,10},{10,8},{9,1... | collective-permute-start | bytes 983048 | tf_op jit(solution)/shard_map/ppermute | solution.py:35
  7.2 1.9 %collective-permute-start = (bf16[40,4096]{1,0:T(8,128)(2,1)}, bf16[40,4096]{1,0:T(8,128)(2,1)S(1)}, u32[]{:S(2)}, u32[]{:S(2)}) collective-permute-start(bf16[40,4096]{1,0:T(8,128)(2,1)} %bitcast.13), channel_id=1, source_target_pairs={{0,8},{12,4},{1,9},{13,5},{2,10},{14,6},{3,11},{15,7},{16,24},{28,... | collective-permute-start | bytes 983048 | tf_op jit(solution)/shard_map/ppermute | solution.py:35
  9.1 4.1 %collective-permute-start.3 = (bf16[40,4096]{1,0:T(8,128)(2,1)}, bf16[40,4096]{1,0:T(8,128)(2,1)S(1)}, u32[]{:S(2)}, u32[]{:S(2)}) collective-permute-start(bf16[40,4096]{1,0:T(8,128)(2,1)} %bitcast.14), channel_id=1, source_target_pairs={{0,12},{12,0},{1,13},{13,1},{2,14},{14,2},{3,15},{15,3},{16,28},{2... | collective-permute-start | bytes 983048 | tf_op jit(solution)/shard_map/ppermute | solution.py:35
  13.2 1.3 %collective-permute-start.2 = (bf16[40,4096]{1,0:T(8,128)(2,1)S(1)}, bf16[40,4096]{1,0:T(8,128)(2,1)S(1)}, u32[]{:S(2)}, u32[]{:S(2)}) collective-permute-start(bf16[40,4096]{1,0:T(8,128)(2,1)S(1)} %collective-permute-done.1.far_in), channel_id=1, source_target_pairs={{8,12},{4,0},{9,13},{5,1},{10,14},{6,2},{11,15},{7,3},{24,28},{20,... | collective-permute-start | bytes 983048 | tf_op jit(solution)/shard_map/ppermute | solution.py:35
  14.6 0.3 collective-permute-start.9
  16.8 2.8 %load.1 = (f32[8,256]{1,0:T(8,128)S(1)}, f32[24,128]{1,0:T(8,128)S(1)}, bf16[40,4096]{1,0:T(8,128)(2,1)S(1)}, bf16[40,4096]{1,0:T(8,128)(2,1)S(1)}, bf16[40,4096...) custom-call(s32[1]{0:T(128)S(6)} %copy.12.ref_len, ...), custom_call_target="tpu_custom_call" | custom-call | flops 10000000 | bytes 4194304 | tf_op jit(solution)/shard_map/load/pallas_call | solution.py:291
  19.6 2.0 %shard_map.113 = (bf16[80,12288]{1,0:T(8,128)(2,1)S(1)}, f32[80,128]{1,0:T(8,128)S(1)}, f32[80,128]{1,0:T(8,128)S(1)}, bf16[80,4096]{1,0:T(8,128)(2,1)S(1)}) custom-call(bf16[40,4096]{1,0:T(8,128)(2,1)S(1)} %get-tuple-element.26.own, bf16[40,4096]{1,0:T(8,128)(2,1)S(1)} %collective-permute-done.4.near, bf16[40,4096]{1,0:T(8,128)(2,1)S(1)} %get-tuple-element.27.k0, ...), custom_call_target="tpu_custom_call" | custom-call | flops 220200960 | tf_op jit(solution)/shard_map/pallas_call | solution.py:265
  21.6 6.5 %collective-permute-done.3.far_out = bf16[40,4096]{1,0:T(8,128)(2,1)S(1)} collective-permute-done((bf16[40,4096]{1,0:T(8,128)(2,1)}, bf16[40,4096]{1,0:T(8,128)(2,1)S(1)}, u32[]{:S(2)}, u32[]{:S(2)}) %collective-permute-start.3) | collective-permute-done | bytes 327712 | tf_op jit(solution)/shard_map/ppermute | solution.py:35
  28.2 2.0 %shard_map.114 = (bf16[80,12288]{1,0:T(8,128)(2,1)S(1)}, f32[80,128]{1,0:T(8,128)S(1)}, f32[80,128]{1,0:T(8,128)S(1)}) custom-call(bf16[40,4096]{1,0:T(8,128)(2,1)S(1)} %collective-permute-done.mid_in, bf16[40,4096]{1,0:T(8,128)(2,1)S(1)} %collective-permute-done.2.mid_out, bf16[40,4096]{1,0:T(8,128)(2,1)S(1)} %collective-permute-done.1.far_in, ...), custom_call_target="tpu_custom_call" | custom-call | flops 220200960 | tf_op jit(solution)/shard_map/pallas_call | solution.py:265
  30.2 0.1 collective-permute-start.6
  30.3 2.5 %collective-permute-start.7 = (f32[80,128]{1,0:T(8,128)S(1)}, f32[80,128]{1,0:T(8,128)S(1)}, u32[]{:S(2)}, u32[]{:S(2)}) collective-permute-start(f32[80,128]{1,0:T(8,128)S(1)} %get-tuple-element.33.own), channel_id=1, source_target_pairs={{0,8},{4,12},{8,0},{12,4},{1,9},{5,13},{9,1},{13,5},{2,10},{6,14},... | collective-permute-start | bytes 122888 | tf_op jit(solution)/shard_map/ppermute | solution.py:35
  32.8 1.1 %collective-permute-start.8 = (f32[80,128]{1,0:T(8,128)S(1)}, f32[80,128]{1,0:T(8,128)S(1)}, u32[]{:S(2)}, u32[]{:S(2)}) collective-permute-start(f32[80,128]{1,0:T(8,128)S(1)} %get-tuple-element.33.own), channel_id=1, source_target_pairs={{0,12},{4,8},{8,4},{12,0},{1,13},{5,9},{9,5},{13,1},{2,14},{6,10},... | collective-permute-start | bytes 122888 | tf_op jit(solution)/shard_map/ppermute | solution.py:35
  33.8 1.5 %shard_map.115 = (f32[4096,80]{1,0:T(8,128)S(1)}, bf16[80,4096]{1,0:T(8,128)(2,1)S(1)}) custom-call(bf16[80,12288]{1,0:T(8,128)(2,1)S(1)} %get-tuple-element.35.exps, bf16[40,4096]{1,0:T(8,128)(2,1)S(1)} %get-tuple-element.36.v0, bf16[40,4096]{1,0:T(8,128)(2,1)S(1)} %collective-permute-done.9.v1, bf16[256,4096]{1,0:T(8,128)(2,1)S(1)} %get-tuple-element.37.refv, ...), custom_call_target="tpu_custom_call" | custom-call | flops 220200960 | tf_op jit(solution)/shard_map/pallas_call | solution.py:265
  35.3 1.4 %shard_map.116.late = f32[4096,80]{1,0:T(8,128)S(1)} custom-call(bf16[80,12288]{1,0:T(8,128)(2,1)S(1)} %get-tuple-element.40.exps, bf16[80,4096]{1,0:T(8,128)(2,1)S(1)} %get-tuple-element.41.values, bf16[256,4096]{1,0:T(8,128)(2,1)S(1)} %get-tuple-element.37.refv, bf16[128,8192]{1,0:T(8,128)(2,1)S(1)} %get-tuple-element.38.weight), custom_call_target="tpu_custom_call" | custom-call | flops 220200960 | tf_op jit(solution)/shard_map/pallas_call | solution.py:265
  36.7 0.7 %collective-permute-done.8.o3 = f32[80,128]{1,0:T(8,128)S(1)} collective-permute-done((f32[80,128]{1,0:T(8,128)S(1)}, f32[80,128]{1,0:T(8,128)S(1)}, u32[]{:S(2)}, u32[]{:S(2)}) %collective-permute-start.8) | collective-permute-done | bytes 40992 | tf_op jit(solution)/shard_map/ppermute | solution.py:35
  37.5 0.7 %shard_map.117 = (f32[20,128]{1,0:T(8,128)S(1)}, f32[20,128]{1,0:T(8,128)S(1)}, f32[20,128]{1,0:T(8,128)S(1)}, f32[20,128]{1,0:T(8,128)S(1)}) custom-call(f32[24,128]{1,0:T(8,128)S(1)} %get-tuple-element.25.scalars, f32[80,128]{1,0:T(8,128)S(1)} %get-tuple-element.33.own, f32[80,128]{1,0:T(8,128)S(1)} %collective-permute-done.6.o1, ...), custom_call_target="tpu_custom_call" | custom-call | tf_op jit(solution)/shard_map/pallas_call | solution.py:265
  38.2 1.8 %collective-permute-start.11 = (f32[20,128]{1,0:T(8,128)S(1)}, f32[20,128]{1,0:T(8,128)S(1)}, u32[]{:S(2)}, u32[]{:S(2)}) collective-permute-start(f32[20,128]{1,0:T(8,128)S(1)} %get-tuple-element.44), channel_id=1, source_target_pairs={{0,8},{4,12},{8,0},{12,4},{1,9},{5,13},{9,1},{13,5},{2,10},{6,14},... | collective-permute-start | bytes 30728 | tf_op jit(solution)/shard_map/ppermute | solution.py:35
  39.9 1.8 %collective-permute-start.12 = (f32[20,128]{1,0:T(8,128)S(1)}, f32[20,128]{1,0:T(8,128)S(1)}, u32[]{:S(2)}, u32[]{:S(2)}) collective-permute-start(f32[20,128]{1,0:T(8,128)S(1)} %get-tuple-element.45), channel_id=1, source_target_pairs={{0,12},{4,8},{8,4},{12,0},{1,13},{5,9},{9,5},{13,1},{2,14},{6,10},... | collective-permute-start | bytes 30728 | tf_op jit(solution)/shard_map/ppermute | solution.py:35
  41.7 2.6 %collective-permute-done.12.r3 = f32[20,128]{1,0:T(8,128)S(1)} collective-permute-done((f32[20,128]{1,0:T(8,128)S(1)}, f32[20,128]{1,0:T(8,128)S(1)}, u32[]{:S(2)}, u32[]{:S(2)}) %collective-permute-start.12) | collective-permute-done | bytes 10272 | tf_op jit(solution)/shard_map/ppermute | solution.py:35
  44.3 7.1 %collective-permute-start.13 = (f32[10,128]{1,0:T(8,128)S(1)}, f32[10,128]{1,0:T(8,128)S(1)}, u32[]{:S(2)}, u32[]{:S(2)}) collective-permute-start(f32[10,128]{1,0:T(8,128)S(1)} %get-tuple-element.47), channel_id=1, source_target_pairs={{0,1},{1,0},{2,3},{3,2},{4,5},{5,4},{6,7},{7,6},{8,9},{9,8},{10,11... | collective-permute-start | bytes 15368 | tf_op jit(solution)/shard_map/ppermute | solution.py:35
  51.5 0.8 %collective-permute-done.13.taken = f32[10,128]{1,0:T(8,128)S(1)} collective-permute-done((f32[10,128]{1,0:T(8,128)S(1)}, f32[10,128]{1,0:T(8,128)S(1)}, u32[]{:S(2)}, u32[]{:S(2)}) %collective-permute-start.13) | collective-permute-done | bytes 5152 | tf_op jit(solution)/shard_map/ppermute | solution.py:35
  52.3 0.6 %shard_map.119 = (f32[10,128]{1,0:T(8,128)}, f32[10,128]{1,0:T(8,128)}) custom-call(f32[24,128]{1,0:T(8,128)S(1)} %get-tuple-element.25.scalars, f32[10,128]{1,0:T(8,128)S(1)} %copy-done, f32[10,128]{1,0:T(8,128)S(1)} %get-tuple-element.46.kept, f32[10,128]{1,0:T(8,128)S(1)} %collective-permute-done.13.taken), custom_call_target="tpu_custom_call" | custom-call | tf_op jit(solution)/shard_map/pallas_call | solution.py:265
  (14 shorter events, 0.1 us)
Async XLA Ops:
  0.6 12.6 %collective-permute-start.1 = (bf16[40,4096]{1,0:T(8,128)(2,1)}, bf16[40,4096]{1,0:T(8,128)(2,1)S(1)}, u32[]{:S(2)}, u32[]{:S(2)}) collective-permute-start(bf16[40,4096]{1,0:T(8,128)(2,1)} %bitcast.11), channel_id=1, source_target_pairs={{4,8},{8,4},{5,9},{9,5},{6,10},{10,6},{7,11},{11,7},{20,24},{24,20... | collective-permute-start | bytes 983048 | tf_op jit(solution)/shard_map/ppermute | solution.py:35
  1.3 13.2 %collective-permute-start.4 = (bf16[40,4096]{1,0:T(8,128)(2,1)}, bf16[40,4096]{1,0:T(8,128)(2,1)S(1)}, u32[]{:S(2)}, u32[]{:S(2)}) collective-permute-start(bf16[40,4096]{1,0:T(8,128)(2,1)} %bitcast.12), channel_id=1, source_target_pairs={{0,4},{4,0},{8,12},{12,8},{1,5},{5,1},{9,13},{13,9},{2,6},{6,2},{1... | collective-permute-start | bytes 983048 | tf_op jit(solution)/shard_map/ppermute | solution.py:35
  6.0 13.6 %collective-permute-start.5 = (bf16[40,4096]{1,0:T(8,128)(2,1)}, bf16[40,4096]{1,0:T(8,128)(2,1)S(1)}, u32[]{:S(2)}, u32[]{:S(2)}) collective-permute-start(bf16[40,4096]{1,0:T(8,128)(2,1)} %bitcast.9), channel_id=1, source_target_pairs={{0,2},{2,0},{1,3},{3,1},{4,6},{6,4},{5,7},{7,5},{8,10},{10,8},{9,1... | collective-permute-start | bytes 983048 | tf_op jit(solution)/shard_map/ppermute | solution.py:35
  7.2 14.4 %collective-permute-start = (bf16[40,4096]{1,0:T(8,128)(2,1)}, bf16[40,4096]{1,0:T(8,128)(2,1)S(1)}, u32[]{:S(2)}, u32[]{:S(2)}) collective-permute-start(bf16[40,4096]{1,0:T(8,128)(2,1)} %bitcast.13), channel_id=1, source_target_pairs={{0,8},{12,4},{1,9},{13,5},{2,10},{14,6},{3,11},{15,7},{16,24},{28,... | collective-permute-start | bytes 983048 | tf_op jit(solution)/shard_map/ppermute | solution.py:35
  9.1 19.1 %collective-permute-start.3 = (bf16[40,4096]{1,0:T(8,128)(2,1)}, bf16[40,4096]{1,0:T(8,128)(2,1)S(1)}, u32[]{:S(2)}, u32[]{:S(2)}) collective-permute-start(bf16[40,4096]{1,0:T(8,128)(2,1)} %bitcast.14), channel_id=1, source_target_pairs={{0,12},{12,0},{1,13},{13,1},{2,14},{14,2},{3,15},{15,3},{16,28},{2... | collective-permute-start | bytes 983048 | tf_op jit(solution)/shard_map/ppermute | solution.py:35
  13.2 15.0 %collective-permute-start.2 = (bf16[40,4096]{1,0:T(8,128)(2,1)S(1)}, bf16[40,4096]{1,0:T(8,128)(2,1)S(1)}, u32[]{:S(2)}, u32[]{:S(2)}) collective-permute-start(bf16[40,4096]{1,0:T(8,128)(2,1)S(1)} %collective-permute-done.1.far_in), channel_id=1, source_target_pairs={{8,12},{4,0},{9,13},{5,1},{10,14},{6,2},{11,15},{7,3},{24,28},{20,... | collective-permute-start | bytes 983048 | tf_op jit(solution)/shard_map/ppermute | solution.py:35
  14.6 19.3 %collective-permute-start.9 = (bf16[40,4096]{1,0:T(8,128)(2,1)}, bf16[40,4096]{1,0:T(8,128)(2,1)S(1)}, u32[]{:S(2)}, u32[]{:S(2)}) collective-permute-start(bf16[40,4096]{1,0:T(8,128)(2,1)} %bitcast.16), channel_id=1, source_target_pairs={{0,2},{2,0},{1,3},{3,1},{4,6},{6,4},{5,7},{7,5},{8,10},{10,8},{9,1... | collective-permute-start | bytes 983048 | tf_op jit(solution)/shard_map/ppermute | solution.py:35
  30.2 6.5 %collective-permute-start.6 = (f32[80,128]{1,0:T(8,128)S(1)}, f32[80,128]{1,0:T(8,128)S(1)}, u32[]{:S(2)}, u32[]{:S(2)}) collective-permute-start(f32[80,128]{1,0:T(8,128)S(1)} %get-tuple-element.33.own), channel_id=1, source_target_pairs={{0,4},{4,0},{8,12},{12,8},{1,5},{5,1},{9,13},{13,9},{2,6},{6,2},{1... | collective-permute-start | bytes 122888 | tf_op jit(solution)/shard_map/ppermute | solution.py:35
  30.3 6.4 %collective-permute-start.7 = (f32[80,128]{1,0:T(8,128)S(1)}, f32[80,128]{1,0:T(8,128)S(1)}, u32[]{:S(2)}, u32[]{:S(2)}) collective-permute-start(f32[80,128]{1,0:T(8,128)S(1)} %get-tuple-element.33.own), channel_id=1, source_target_pairs={{0,8},{4,12},{8,0},{12,4},{1,9},{5,13},{9,1},{13,5},{2,10},{6,14},... | collective-permute-start | bytes 122888 | tf_op jit(solution)/shard_map/ppermute | solution.py:35
  32.8 4.7 %collective-permute-start.8 = (f32[80,128]{1,0:T(8,128)S(1)}, f32[80,128]{1,0:T(8,128)S(1)}, u32[]{:S(2)}, u32[]{:S(2)}) collective-permute-start(f32[80,128]{1,0:T(8,128)S(1)} %get-tuple-element.33.own), channel_id=1, source_target_pairs={{0,12},{4,8},{8,4},{12,0},{1,13},{5,9},{9,5},{13,1},{2,14},{6,10},... | collective-permute-start | bytes 122888 | tf_op jit(solution)/shard_map/ppermute | solution.py:35
  37.5 14.8 %copy-start = (f32[10,128]{1,0:T(8,128)S(1)}, f32[10,128]{1,0:T(8,128)}, u32[]{:S(2)}) copy-start(f32[10,128]{1,0:T(8,128)} %latent.1) | copy-start | bytes 15364
  38.1 3.6 %collective-permute-start.10 = (f32[20,128]{1,0:T(8,128)S(1)}, f32[20,128]{1,0:T(8,128)S(1)}, u32[]{:S(2)}, u32[]{:S(2)}) collective-permute-start(f32[20,128]{1,0:T(8,128)S(1)} %get-tuple-element.43), channel_id=1, source_target_pairs={{0,4},{4,0},{8,12},{12,8},{1,5},{5,1},{9,13},{13,9},{2,6},{6,2},{1... | collective-permute-start | bytes 30728 | tf_op jit(solution)/shard_map/ppermute | solution.py:35
  38.2 3.5 %collective-permute-start.11 = (f32[20,128]{1,0:T(8,128)S(1)}, f32[20,128]{1,0:T(8,128)S(1)}, u32[]{:S(2)}, u32[]{:S(2)}) collective-permute-start(f32[20,128]{1,0:T(8,128)S(1)} %get-tuple-element.44), channel_id=1, source_target_pairs={{0,8},{4,12},{8,0},{12,4},{1,9},{5,13},{9,1},{13,5},{2,10},{6,14},... | collective-permute-start | bytes 30728 | tf_op jit(solution)/shard_map/ppermute | solution.py:35
  39.9 4.3 %collective-permute-start.12 = (f32[20,128]{1,0:T(8,128)S(1)}, f32[20,128]{1,0:T(8,128)S(1)}, u32[]{:S(2)}, u32[]{:S(2)}) collective-permute-start(f32[20,128]{1,0:T(8,128)S(1)} %get-tuple-element.45), channel_id=1, source_target_pairs={{0,12},{4,8},{8,4},{12,0},{1,13},{5,9},{9,5},{13,1},{2,14},{6,10},... | collective-permute-start | bytes 30728 | tf_op jit(solution)/shard_map/ppermute | solution.py:35
  44.3 8.0 %collective-permute-start.13 = (f32[10,128]{1,0:T(8,128)S(1)}, f32[10,128]{1,0:T(8,128)S(1)}, u32[]{:S(2)}, u32[]{:S(2)}) collective-permute-start(f32[10,128]{1,0:T(8,128)S(1)} %get-tuple-element.47), channel_id=1, source_target_pairs={{0,1},{1,0},{2,3},{3,2},{4,5},{5,4},{6,7},{7,6},{8,9},{9,8},{10,11... | collective-permute-start | bytes 15368 | tf_op jit(solution)/shard_map/ppermute | solution.py:35
where the time goes:
time: 53.4 us; the launch traced here: 52.9 us
  starting transfers between devices  28.5 us (53%)
  Pallas kernels  10.9 us (20%)
  waiting for transfers between devices  10.7 us (20%)
  between operations  2.72 us (5%)
    ppermute x14, starting transfers between devices, exchange(): return lax.ppermute(value, axis, pairs)  28.5 us
    ppermute x14, waiting for transfers between devices, exchange(): return lax.ppermute(value, axis, pairs)  10.7 us
    pallas_call x7, Pallas kernels, call(): pl.pallas_call(kernel, in_specs=[VMEM] * len(arrays), out_specs=[VMEM] *...  8.17 us
    pallas_call x1, Pallas kernels, line_of_four(): pl.pallas_call(partial(load_kernel, heads), in_specs=[SMEM] * 3 + [pl.Blo...  2.77 us
  transfers between devices with their start and end apart: 14, of which 4 were waited for; matrix products, arithmetic and copies ran while one was open for 0% of the time, Pallas kernels for 18%

commit v1 on v0

--- a/solution.py
+++ b/solution.py
@@ -180,30 +180,47 @@
     value_rows(heads, exps, values, refv, weight, out)
 
 
-def late_scores_kernel(
-    heads, mid_in, mid_out, far_in, far_out, keys, refk, bias, lse_early, top_early,
+def far_scores_kernel(heads, far_in, far_out, keys, refk, bias, exps, lse, top, query):
+    @pl.when(is_inner())
+    def _():
+        query[...] = far_in[...]
+
+    @pl.when(jnp.logical_not(is_inner()))
+    def _():
+        query[...] = far_out[...]
+
+    lse[...], top[...] = score_rows(heads, query, keys, refk, bias, exps)
+
+
+def middle_scores_kernel(
+    heads, mid_in, mid_out, keys, refk, bias, lse_early, top_early, lse_far, top_far,
     exps, lse, top, query,
 ):
     @pl.when(is_inner())
     def _():
-        fill_rows(query, (mid_in, far_in))
+        query[...] = mid_in[...]
 
     @pl.when(jnp.logical_not(is_inner()))
     def _():
-        fill_rows(query, (mid_out, far_out))
-
-    low = lax.broadcasted_iota(jnp.int32, lse.shape, 1) < 64
-    late = score_rows(heads, query, keys, refk, bias, exps)
-    for out, early, mine in ((lse, lse_early, late[0]), (top, top_early, late[1])):
-        out[...] = jnp.where(low, early[...], pltpu.roll(mine, 64, 1))
-
-
-def late_values_kernel(heads, exps, values, refv, weight, out):
+        query[...] = mid_out[...]
+
+    count = query.shape[0]
+    low = lax.broadcasted_iota(jnp.int32, (count, 128), 1) < 64
+    far_lse, far_top = pltpu.roll(lse_far[...], 64, 1), pltpu.roll(top_far[...], 64, 1)
+    lse[count:] = jnp.where(low, lse_early[count:], far_lse)
+    top[count:] = jnp.where(low, top_early[count:], far_top)
+    found = score_rows(heads, query, keys, refk, bias, exps)
+    lse[:count] = jnp.where(low, lse_early[:count], pltpu.roll(found[0], 64, 1))
+    top[:count] = jnp.where(low, top_early[:count], pltpu.roll(found[1], 64, 1))
+
+
+def late_values_kernel(heads, middle, far, values, refv, weight, out, exps):
+    fill_rows(exps, (middle, far))
     value_rows(heads, exps, values, refv, weight, out)
 
 
 def combine_kernel(
-    heads, scalars, own, o1, o2, o3, top, early, late, b0, b1, b2, b3, velocity
+    heads, scalars, own, o1, o2, o3, top, early, late, b0, b1, b2, b3, given, velocity
 ):
     rows = own.shape[0]
     count = rows // 2
@@ -234,7 +251,12 @@
     first = jnp.where(low, even, pltpu.roll(odd, 64, 1))
     second = jnp.where(low, pltpu.roll(even, 64, 1), odd)
     half = count // 2
-    b0[...], b1[...], b2[...], b3[...] = first[:half], first[half:], second[:half], second[half:]
+    blocks = first[:half], first[half:], second[:half], second[half:]
+    cfg = lax.axis_index("cfg") == 0
+    size = half // 2
+    for i, (block, kept) in enumerate(zip(blocks, (b0, b1, b2, b3))):
+        kept[...] = jnp.where(cfg, block[:size], block[size:])
+        given[i * 16 : i * 16 + size, :] = jnp.where(cfg, block[size:], block[:size])
 
 
 def share_of(own, everyone):
@@ -247,16 +269,13 @@
     return jnp.exp2(own - top) * (1.0 / total)
 
 
-def split_kernel(b0, r1, r2, r3, kept, given):
-    total = (b0[...] + r1[...]) + (r2[...] + r3[...])
-    half = total.shape[0] // 2
-    first = lax.axis_index("cfg") == 0
-    kept[...] = jnp.where(first, total[:half], total[half:])
-    given[...] = jnp.where(first, total[half:], total[:half])
-
-
-def euler_kernel(scalars, latent, kept, taken, latent_next, denoised):
-    guided = kept[...] + taken[...]
+def join_kernel(taken, b0, b1, b2, b3, g0, g1, g2, g3):
+    for i, (block, out) in enumerate(((b0, g0), (b1, g1), (b2, g2), (b3, g3))):
+        out[...] = block[...] + taken[i * 16 : i * 16 + out.shape[0], :]
+
+
+def euler_kernel(scalars, latent, own, r1, r2, r3, latent_next, denoised):
+    guided = (own[...] + r1[...]) + (r2[...] + r3[...])
     latent_next[...] = latent[...] + scalars[16:17, :] * guided
     denoised[...] = latent[...] - scalars[8:9, :] * guided
 
@@ -316,31 +335,39 @@
         partial(early_values_kernel, heads),
         (exps_e, values, v_other, refv, weight), [partial_shape, stacked], flops=flops,
     )
-    exps_l, lse, top = call(
-        partial(late_scores_kernel, heads),
-        (mid_in, mid_out, far_in, far_out, keys, refk, bias, lse_e, top_e),
-        [exps_shape, columns, columns], [stacked], flops=flops,
+    small = pltpu.VMEM((count, exps_shape.shape[1]), bf16)
+    column = pltpu.VMEM((count, 128), f32)
+    block_shape = pltpu.VMEM((count, width), bf16)
+    exps_f, lse_f, top_f = call(
+        partial(far_scores_kernel, heads),
+        (far_in, far_out, keys, refk, bias),
+        [small, column, column], [block_shape], flops=flops // 2,
+    )
+    exps_m, lse, top = call(
+        partial(middle_scores_kernel, heads),
+        (mid_in, mid_out, keys, refk, bias, lse_e, top_e, lse_f, top_f),
+        [small, columns, columns], [block_shape], flops=flops // 2,
     )
     o3 = swap(lse, "seq", 3)
     o2 = swap(lse, "seq", 2)
     o1 = swap(lse, "seq", 1)
     (late,) = call(
         partial(late_values_kernel, heads),
-        (exps_l, values, refv, weight), [partial_shape], flops=flops,
-    )
-    block = pltpu.VMEM((count // 2, 128), f32)
-    blocks = call(
+        (exps_m, exps_f, values, refv, weight), [partial_shape], [exps_shape], flops=flops,
+    )
+    half = pltpu.VMEM(latent.shape, f32)
+    *kept, given = call(
         partial(combine_kernel, heads),
-        (scalars, lse, o1, o2, o3, top, early, late), [block] * 4, [columns],
-    )
+        (scalars, lse, o1, o2, o3, top, early, late),
+        [half] * 4 + [pltpu.VMEM((64, 128), f32)], [columns],
+    )
+    taken = swap(given, "cfg", 1)
+    blocks = call(join_kernel, (taken, *kept), [half] * 4, mib=2)
     r3 = swap(blocks[3], "seq", 3)
     r2 = swap(blocks[2], "seq", 2)
     r1 = swap(blocks[1], "seq", 1)
-    half = pltpu.VMEM(latent.shape, latent.dtype)
-    kept, given = call(split_kernel, (blocks[0], r1, r2, r3), [half] * 2, mib=2)
-    taken = swap(given, "cfg", 1)
     result = jax.ShapeDtypeStruct(latent.shape, latent.dtype)
-    return call(euler_kernel, (scalars, latent, kept, taken), [result] * 2, mib=2)
+    return call(euler_kernel, (scalars, latent, blocks[0], r1, r2, r3), [result] * 2, mib=2)
 
 
 def attend_kernel(heads, valid, query, keys, values, refk, refv, w_ref, out, lse, share, weight):

time: 53.4 us -> 49.9 us (0.934)
  the two profiles are of different devices: /device:TPU:1 before, /device:TPU:0 now
where the time goes in v1:
time: 49.9 us; the launch traced here: 49.7 us
  starting transfers between devices  24.3 us (49%)
  Pallas kernels  11.5 us (23%)
  waiting for transfers between devices  11.2 us (22%)
  between operations  2.7 us (5%)
    ppermute x14, starting transfers between devices, exchange(): return lax.ppermute(value, axis, pairs)  24.3 us
    ppermute x14, waiting for transfers between devices, exchange(): return lax.ppermute(value, axis, pairs)  11.2 us
    pallas_call x8, Pallas kernels, call(): pl.pallas_call(kernel, in_specs=[VMEM] * len(arrays), out_specs=[VMEM] *...  8.69 us
    pallas_call x1, Pallas kernels, line_of_four(): pl.pallas_call(partial(load_kernel, heads), in_specs=[SMEM] * 3 + [pl.Blo...  2.77 us
  transfers between devices with their start and end apart: 14, of which 8 were waited for; matrix products, arithmetic and copies ran while one was open for 0% of the time, Pallas kernels for 20%

profile of v1, /device:TPU:0, one launch (start us, length us, event | category | flops | bytes accessed | tf_op | source)
XLA Modules:
  0.0 49.7 jit_solution(10625388817477116988)
XLA Ops:
  0.6 0.7 %collective-permute-start.1 = (bf16[40,4096]{1,0:T(8,128)(2,1)}, bf16[40,4096]{1,0:T(8,128)(2,1)S(1)}, u32[]{:S(2)}, u32[]{:S(2)}) collective-permute-start(bf16[40,4096]{1,0:T(8,128)(2,1)} %bitcast.11), channel_id=1, source_target_pairs={{4,8},{8,4},{5,9},{9,5},{6,10},{10,6},{7,11},{11,7},{20,24},{24,20... | collective-permute-start | bytes 983048 | tf_op jit(solution)/shard_map/ppermute | solution.py:35
  1.3 5.9 %collective-permute-start.3 = (bf16[40,4096]{1,0:T(8,128)(2,1)}, bf16[40,4096]{1,0:T(8,128)(2,1)S(1)}, u32[]{:S(2)}, u32[]{:S(2)}) collective-permute-start(bf16[40,4096]{1,0:T(8,128)(2,1)} %bitcast.12), channel_id=1, source_target_pairs={{0,4},{4,0},{8,12},{12,8},{1,5},{5,1},{9,13},{13,9},{2,6},{6,2},{1... | collective-permute-start | bytes 983048 | tf_op jit(solution)/shard_map/ppermute | solution.py:35
  7.2 1.5 %collective-permute-start.4 = (bf16[40,4096]{1,0:T(8,128)(2,1)}, bf16[40,4096]{1,0:T(8,128)(2,1)S(1)}, u32[]{:S(2)}, u32[]{:S(2)}) collective-permute-start(bf16[40,4096]{1,0:T(8,128)(2,1)} %bitcast.9), channel_id=1, source_target_pairs={{0,2},{2,0},{1,3},{3,1},{4,6},{6,4},{5,7},{7,5},{8,10},{10,8},{9,1... | collective-permute-start | bytes 983048 | tf_op jit(solution)/shard_map/ppermute | solution.py:35
  8.7 3.2 %collective-permute-start.5 = (bf16[40,4096]{1,0:T(8,128)(2,1)}, bf16[40,4096]{1,0:T(8,128)(2,1)S(1)}, u32[]{:S(2)}, u32[]{:S(2)}) collective-permute-start(bf16[40,4096]{1,0:T(8,128)(2,1)} %bitcast.13), channel_id=1, source_target_pairs={{0,12},{12,0},{1,13},{13,1},{2,14},{14,2},{3,15},{15,3},{16,28},{2... | collective-permute-start | bytes 983048 | tf_op jit(solution)/shard_map/ppermute | solution.py:35
  12.0 1.3 %collective-permute-start = (bf16[40,4096]{1,0:T(8,128)(2,1)}, bf16[40,4096]{1,0:T(8,128)(2,1)S(1)}, u32[]{:S(2)}, u32[]{:S(2)}) collective-permute-start(bf16[40,4096]{1,0:T(8,128)(2,1)} %bitcast.14), channel_id=1, source_target_pairs={{0,8},{12,4},{1,9},{13,5},{2,10},{14,6},{3,11},{15,7},{16,24},{28,... | collective-permute-start | bytes 983048 | tf_op jit(solution)/shard_map/ppermute | solution.py:35
  13.3 1.3 %collective-permute-start.2 = (bf16[40,4096]{1,0:T(8,128)(2,1)S(1)}, bf16[40,4096]{1,0:T(8,128)(2,1)S(1)}, u32[]{:S(2)}, u32[]{:S(2)}) collective-permute-start(bf16[40,4096]{1,0:T(8,128)(2,1)S(1)} %collective-permute-done.1.far_in), channel_id=1, source_target_pairs={{8,12},{4,0},{9,13},{5,1},{10,14},{6,2},{11,15},{7,3},{24,28},{20,... | collective-permute-start | bytes 983048 | tf_op jit(solution)/shard_map/ppermute | solution.py:35
  14.6 1.0 %collective-permute-done.3.near = bf16[40,4096]{1,0:T(8,128)(2,1)S(1)} collective-permute-done((bf16[40,4096]{1,0:T(8,128)(2,1)}, bf16[40,4096]{1,0:T(8,128)(2,1)S(1)}, u32[]{:S(2)}, u32[]{:S(2)}) %collective-permute-start.3) | collective-permute-done | bytes 327712 | tf_op jit(solution)/shard_map/ppermute | solution.py:35
  15.7 1.5 %collective-permute-start.9 = (bf16[40,4096]{1,0:T(8,128)(2,1)}, bf16[40,4096]{1,0:T(8,128)(2,1)S(1)}, u32[]{:S(2)}, u32[]{:S(2)}) collective-permute-start(bf16[40,4096]{1,0:T(8,128)(2,1)} %bitcast.16), channel_id=1, source_target_pairs={{0,2},{2,0},{1,3},{3,1},{4,6},{6,4},{5,7},{7,5},{8,10},{10,8},{9,1... | collective-permute-start | bytes 983048 | tf_op jit(solution)/shard_map/ppermute | solution.py:35
  19.1 2.8 %load.1 = (f32[8,256]{1,0:T(8,128)S(1)}, f32[24,128]{1,0:T(8,128)S(1)}, bf16[40,4096]{1,0:T(8,128)(2,1)S(1)}, bf16[40,4096]{1,0:T(8,128)(2,1)S(1)}, bf16[40,4096...) custom-call(s32[1]{0:T(128)S(6)} %copy.12.ref_len, ...), custom_call_target="tpu_custom_call" | custom-call | flops 10000000 | bytes 4194304 | tf_op jit(solution)/shard_map/load/pallas_call | solution.py:310
  21.9 2.0 %shard_map.113 = (bf16[80,12288]{1,0:T(8,128)(2,1)S(1)}, f32[80,128]{1,0:T(8,128)S(1)}, f32[80,128]{1,0:T(8,128)S(1)}, bf16[80,4096]{1,0:T(8,128)(2,1)S(1)}) custom-call(bf16[40,4096]{1,0:T(8,128)(2,1)S(1)} %get-tuple-element.32.own, bf16[40,4096]{1,0:T(8,128)(2,1)S(1)} %collective-permute-done.3.near, bf16[40,4096]{1,0:T(8,128)(2,1)S(1)} %get-tuple-element.33.k0, ...), custom_call_target="tpu_custom_call" | custom-call | flops 220200960 | tf_op jit(solution)/shard_map/pallas_call | solution.py:284
  24.4 1.2 %shard_map.114 = (bf16[40,12288]{1,0:T(8,128)(2,1)S(1)}, f32[40,128]{1,0:T(8,128)S(1)}, f32[40,128]{1,0:T(8,128)S(1)}) custom-call(bf16[40,4096]{1,0:T(8,128)(2,1)S(1)} %collective-permute-done.1.far_in, bf16[40,4096]{1,0:T(8,128)(2,1)S(1)} %collective-permute-done.5.far_out, bf16[80,4096]{1,0:T(8,128)(2,1)S(1)} %get-tuple-element.36.keys, ...), custom_call_target="tpu_custom_call" | custom-call | flops 110100480 | tf_op jit(solution)/shard_map/pallas_call | solution.py:284
  25.6 2.7 %collective-permute-done.mid_in = bf16[40,4096]{1,0:T(8,128)(2,1)S(1)} collective-permute-done((bf16[40,4096]{1,0:T(8,128)(2,1)}, bf16[40,4096]{1,0:T(8,128)(2,1)S(1)}, u32[]{:S(2)}, u32[]{:S(2)}) %collective-permute-start) | collective-permute-done | bytes 327712 | tf_op jit(solution)/shard_map/ppermute | solution.py:35
  28.3 1.3 %collective-permute-done.2.mid_out = bf16[40,4096]{1,0:T(8,128)(2,1)S(1)} collective-permute-done((bf16[40,4096]{1,0:T(8,128)(2,1)S(1)}, bf16[40,4096]{1,0:T(8,128)(2,1)S(1)}, u32[]{:S(2)}, u32[]{:S(2)}) %collective-permute-start.2) | collective-permute-done | bytes 327712 | tf_op jit(solution)/shard_map/ppermute | solution.py:35
  29.6 1.3 %shard_map.115 = (bf16[40,12288]{1,0:T(8,128)(2,1)S(1)}, f32[80,128]{1,0:T(8,128)S(1)}, f32[80,128]{1,0:T(8,128)S(1)}) custom-call(bf16[40,4096]{1,0:T(8,128)(2,1)S(1)} %collective-permute-done.mid_in, bf16[40,4096]{1,0:T(8,128)(2,1)S(1)} %collective-permute-done.2.mid_out, bf16[80,4096]{1,0:T(8,128)(2,1)S(1)} %get-tuple-element.36.keys, ...), custom_call_target="tpu_custom_call" | custom-call | flops 110100480 | tf_op jit(solution)/shard_map/pallas_call | solution.py:284
  30.9 1.1 %collective-permute-start.6 = (f32[80,128]{1,0:T(8,128)S(1)}, f32[80,128]{1,0:T(8,128)S(1)}, u32[]{:S(2)}, u32[]{:S(2)}) collective-permute-start(f32[80,128]{1,0:T(8,128)S(1)} %get-tuple-element.41.own), channel_id=1, source_target_pairs={{0,4},{4,0},{8,12},{12,8},{1,5},{5,1},{9,13},{13,9},{2,6},{6,2},{1... | collective-permute-start | bytes 122888 | tf_op jit(solution)/shard_map/ppermute | solution.py:35
  31.9 2.0 %collective-permute-start.7 = (f32[80,128]{1,0:T(8,128)S(1)}, f32[80,128]{1,0:T(8,128)S(1)}, u32[]{:S(2)}, u32[]{:S(2)}) collective-permute-start(f32[80,128]{1,0:T(8,128)S(1)} %get-tuple-element.41.own), channel_id=1, source_target_pairs={{0,8},{4,12},{8,0},{12,4},{1,9},{5,13},{9,1},{13,5},{2,10},{6,14},... | collective-permute-start | bytes 122888 | tf_op jit(solution)/shard_map/ppermute | solution.py:35
  34.0 1.3 %collective-permute-start.8 = (f32[80,128]{1,0:T(8,128)S(1)}, f32[80,128]{1,0:T(8,128)S(1)}, u32[]{:S(2)}, u32[]{:S(2)}) collective-permute-start(f32[80,128]{1,0:T(8,128)S(1)} %get-tuple-element.41.own), channel_id=1, source_target_pairs={{0,12},{4,8},{8,4},{12,0},{1,13},{5,9},{9,5},{13,1},{2,14},{6,10},... | collective-permute-start | bytes 122888 | tf_op jit(solution)/shard_map/ppermute | solution.py:35
  35.3 1.4 %shard_map.116 = (f32[4096,80]{1,0:T(8,128)S(1)}, bf16[80,4096]{1,0:T(8,128)(2,1)S(1)}) custom-call(bf16[80,12288]{1,0:T(8,128)(2,1)S(1)} %get-tuple-element.43.exps, bf16[40,4096]{1,0:T(8,128)(2,1)S(1)} %get-tuple-element.44.v0, bf16[40,4096]{1,0:T(8,128)(2,1)S(1)} %collective-permute-done.9.v1, bf16[256,4096]{1,0:T(8,128)(2,1)S(1)} %get-tuple-element.45.refv, ...), custom_call_target="tpu_custom_call" | custom-call | flops 220200960 | tf_op jit(solution)/shard_map/pallas_call | solution.py:284
  36.8 1.4 %shard_map.117.late = f32[4096,80]{1,0:T(8,128)S(1)} custom-call(bf16[40,12288]{1,0:T(8,128)(2,1)S(1)} %get-tuple-element.48.middle, bf16[40,12288]{1,0:T(8,128)(2,1)S(1)} %get-tuple-element.49.far, bf16[80,4096]{1,0:T(8,128)(2,1)S(1)} %get-tuple-element.50.values, bf16[256,4096]{1,0:T(8,128)(2,1)S(1)} %get-tuple-element.45.refv, ...), custom_call_target="tpu_custom_call" | custom-call | flops 220200960 | tf_op jit(solution)/shard_map/pallas_call | solution.py:284
  38.2 1.6 %collective-permute-done.8.o3 = f32[80,128]{1,0:T(8,128)S(1)} collective-permute-done((f32[80,128]{1,0:T(8,128)S(1)}, f32[80,128]{1,0:T(8,128)S(1)}, u32[]{:S(2)}, u32[]{:S(2)}) %collective-permute-start.8) | collective-permute-done | bytes 40992 | tf_op jit(solution)/shard_map/ppermute | solution.py:35
  40.5 1.2 %collective-permute-done.10.taken = f32[64,128]{1,0:T(8,128)S(1)} collective-permute-done((f32[64,128]{1,0:T(8,128)S(1)}, f32[64,128]{1,0:T(8,128)S(1)}, u32[]{:S(2)}, u32[]{:S(2)}) %collective-permute-start.10) | collective-permute-done | bytes 32800 | tf_op jit(solution)/shard_map/ppermute | solution.py:35
  41.7 1.9 %collective-permute-start.12 = (f32[10,128]{1,0:T(8,128)S(1)}, f32[10,128]{1,0:T(8,128)S(1)}, u32[]{:S(2)}, u32[]{:S(2)}) collective-permute-start(f32[10,128]{1,0:T(8,128)S(1)} %get-tuple-element.58), channel_id=1, source_target_pairs={{0,8},{4,12},{8,0},{12,4},{1,9},{5,13},{9,1},{13,5},{2,10},{6,14},... | collective-permute-start | bytes 15368 | tf_op jit(solution)/shard_map/ppermute | solution.py:35
  43.6 2.5 %collective-permute-start.13 = (f32[10,128]{1,0:T(8,128)S(1)}, f32[10,128]{1,0:T(8,128)S(1)}, u32[]{:S(2)}, u32[]{:S(2)}) collective-permute-start(f32[10,128]{1,0:T(8,128)S(1)} %get-tuple-element.59), channel_id=1, source_target_pairs={{0,12},{4,8},{8,4},{12,0},{1,13},{5,9},{9,5},{13,1},{2,14},{6,10},... | collective-permute-start | bytes 15368 | tf_op jit(solution)/shard_map/ppermute | solution.py:35
  46.4 2.7 %collective-permute-done.13.r3 = f32[10,128]{1,0:T(8,128)S(1)} collective-permute-done((f32[10,128]{1,0:T(8,128)S(1)}, f32[10,128]{1,0:T(8,128)S(1)}, u32[]{:S(2)}, u32[]{:S(2)}) %collective-permute-start.13) | collective-permute-done | bytes 5152 | tf_op jit(solution)/shard_map/ppermute | solution.py:35
  (15 shorter events, 2.1 us)
Async XLA Ops:
  0.6 12.7 %collective-permute-start.1 = (bf16[40,4096]{1,0:T(8,128)(2,1)}, bf16[40,4096]{1,0:T(8,128)(2,1)S(1)}, u32[]{:S(2)}, u32[]{:S(2)}) collective-permute-start(bf16[40,4096]{1,0:T(8,128)(2,1)} %bitcast.11), channel_id=1, source_target_pairs={{4,8},{8,4},{5,9},{9,5},{6,10},{10,6},{7,11},{11,7},{20,24},{24,20... | collective-permute-start | bytes 983048 | tf_op jit(solution)/shard_map/ppermute | solution.py:35
  1.3 14.3 %collective-permute-start.3 = (bf16[40,4096]{1,0:T(8,128)(2,1)}, bf16[40,4096]{1,0:T(8,128)(2,1)S(1)}, u32[]{:S(2)}, u32[]{:S(2)}) collective-permute-start(bf16[40,4096]{1,0:T(8,128)(2,1)} %bitcast.12), channel_id=1, source_target_pairs={{0,4},{4,0},{8,12},{12,8},{1,5},{5,1},{9,13},{13,9},{2,6},{6,2},{1... | collective-permute-start | bytes 983048 | tf_op jit(solution)/shard_map/ppermute | solution.py:35
  7.2 14.6 %collective-permute-start.4 = (bf16[40,4096]{1,0:T(8,128)(2,1)}, bf16[40,4096]{1,0:T(8,128)(2,1)S(1)}, u32[]{:S(2)}, u32[]{:S(2)}) collective-permute-start(bf16[40,4096]{1,0:T(8,128)(2,1)} %bitcast.9), channel_id=1, source_target_pairs={{0,2},{2,0},{1,3},{3,1},{4,6},{6,4},{5,7},{7,5},{8,10},{10,8},{9,1... | collective-permute-start | bytes 983048 | tf_op jit(solution)/shard_map/ppermute | solution.py:35
  8.7 15.6 %collective-permute-start.5 = (bf16[40,4096]{1,0:T(8,128)(2,1)}, bf16[40,4096]{1,0:T(8,128)(2,1)S(1)}, u32[]{:S(2)}, u32[]{:S(2)}) collective-permute-start(bf16[40,4096]{1,0:T(8,128)(2,1)} %bitcast.13), channel_id=1, source_target_pairs={{0,12},{12,0},{1,13},{13,1},{2,14},{14,2},{3,15},{15,3},{16,28},{2... | collective-permute-start | bytes 983048 | tf_op jit(solution)/shard_map/ppermute | solution.py:35
  12.0 16.3 %collective-permute-start = (bf16[40,4096]{1,0:T(8,128)(2,1)}, bf16[40,4096]{1,0:T(8,128)(2,1)S(1)}, u32[]{:S(2)}, u32[]{:S(2)}) collective-permute-start(bf16[40,4096]{1,0:T(8,128)(2,1)} %bitcast.14), channel_id=1, source_target_pairs={{0,8},{12,4},{1,9},{13,5},{2,10},{14,6},{3,11},{15,7},{16,24},{28,... | collective-permute-start | bytes 983048 | tf_op jit(solution)/shard_map/ppermute | solution.py:35
  13.3 16.3 %collective-permute-start.2 = (bf16[40,4096]{1,0:T(8,128)(2,1)S(1)}, bf16[40,4096]{1,0:T(8,128)(2,1)S(1)}, u32[]{:S(2)}, u32[]{:S(2)}) collective-permute-start(bf16[40,4096]{1,0:T(8,128)(2,1)S(1)} %collective-permute-done.1.far_in), channel_id=1, source_target_pairs={{8,12},{4,0},{9,13},{5,1},{10,14},{6,2},{11,15},{7,3},{24,28},{20,... | collective-permute-start | bytes 983048 | tf_op jit(solution)/shard_map/ppermute | solution.py:35
  15.7 19.7 %collective-permute-start.9 = (bf16[40,4096]{1,0:T(8,128)(2,1)}, bf16[40,4096]{1,0:T(8,128)(2,1)S(1)}, u32[]{:S(2)}, u32[]{:S(2)}) collective-permute-start(bf16[40,4096]{1,0:T(8,128)(2,1)} %bitcast.16), channel_id=1, source_target_pairs={{0,2},{2,0},{1,3},{3,1},{4,6},{6,4},{5,7},{7,5},{8,10},{10,8},{9,1... | collective-permute-start | bytes 983048 | tf_op jit(solution)/shard_map/ppermute | solution.py:35
  30.9 7.3 %collective-permute-start.6 = (f32[80,128]{1,0:T(8,128)S(1)}, f32[80,128]{1,0:T(8,128)S(1)}, u32[]{:S(2)}, u32[]{:S(2)}) collective-permute-start(f32[80,128]{1,0:T(8,128)S(1)} %get-tuple-element.41.own), channel_id=1, source_target_pairs={{0,4},{4,0},{8,12},{12,8},{1,5},{5,1},{9,13},{13,9},{2,6},{6,2},{1... | collective-permute-start | bytes 122888 | tf_op jit(solution)/shard_map/ppermute | solution.py:35
  31.9 6.3 %collective-permute-start.7 = (f32[80,128]{1,0:T(8,128)S(1)}, f32[80,128]{1,0:T(8,128)S(1)}, u32[]{:S(2)}, u32[]{:S(2)}) collective-permute-start(f32[80,128]{1,0:T(8,128)S(1)} %get-tuple-element.41.own), channel_id=1, source_target_pairs={{0,8},{4,12},{8,0},{12,4},{1,9},{5,13},{9,1},{13,5},{2,10},{6,14},... | collective-permute-start | bytes 122888 | tf_op jit(solution)/shard_map/ppermute | solution.py:35
  34.0 5.8 %collective-permute-start.8 = (f32[80,128]{1,0:T(8,128)S(1)}, f32[80,128]{1,0:T(8,128)S(1)}, u32[]{:S(2)}, u32[]{:S(2)}) collective-permute-start(f32[80,128]{1,0:T(8,128)S(1)} %get-tuple-element.41.own), channel_id=1, source_target_pairs={{0,12},{4,8},{8,4},{12,0},{1,13},{5,9},{9,5},{13,1},{2,14},{6,10},... | collective-permute-start | bytes 122888 | tf_op jit(solution)/shard_map/ppermute | solution.py:35
  39.8 9.3 %copy-start = (f32[10,128]{1,0:T(8,128)S(1)}, f32[10,128]{1,0:T(8,128)}, u32[]{:S(2)}) copy-start(f32[10,128]{1,0:T(8,128)} %latent.1) | copy-start | bytes 15364
  40.5 1.3 %collective-permute-start.10 = (f32[64,128]{1,0:T(8,128)S(1)}, f32[64,128]{1,0:T(8,128)S(1)}, u32[]{:S(2)}, u32[]{:S(2)}) collective-permute-start(f32[64,128]{1,0:T(8,128)S(1)} %get-tuple-element.51), channel_id=1, source_target_pairs={{0,1},{1,0},{2,3},{3,2},{4,5},{5,4},{6,7},{7,6},{8,9},{9,8},{10,11... | collective-permute-start | bytes 98312 | tf_op jit(solution)/shard_map/ppermute | solution.py:35
  41.7 4.4 %collective-permute-start.11 = (f32[10,128]{1,0:T(8,128)S(1)}, f32[10,128]{1,0:T(8,128)S(1)}, u32[]{:S(2)}, u32[]{:S(2)}) collective-permute-start(f32[10,128]{1,0:T(8,128)S(1)} %get-tuple-element.57), channel_id=1, source_target_pairs={{0,4},{4,0},{8,12},{12,8},{1,5},{5,1},{9,13},{13,9},{2,6},{6,2},{1... | collective-permute-start | bytes 15368 | tf_op jit(solution)/shard_map/ppermute | solution.py:35
  41.7 4.6 %collective-permute-start.12 = (f32[10,128]{1,0:T(8,128)S(1)}, f32[10,128]{1,0:T(8,128)S(1)}, u32[]{:S(2)}, u32[]{:S(2)}) collective-permute-start(f32[10,128]{1,0:T(8,128)S(1)} %get-tuple-element.58), channel_id=1, source_target_pairs={{0,8},{4,12},{8,0},{12,4},{1,9},{5,13},{9,1},{13,5},{2,10},{6,14},... | collective-permute-start | bytes 15368 | tf_op jit(solution)/shard_map/ppermute | solution.py:35
  43.6 5.4 %collective-permute-start.13 = (f32[10,128]{1,0:T(8,128)S(1)}, f32[10,128]{1,0:T(8,128)S(1)}, u32[]{:S(2)}, u32[]{:S(2)}) collective-permute-start(f32[10,128]{1,0:T(8,128)S(1)} %get-tuple-element.59), channel_id=1, source_target_pairs={{0,12},{4,8},{8,4},{12,0},{1,13},{5,9},{9,5},{13,1},{2,14},{6,10},... | collective-permute-start | bytes 15368 | tf_op jit(solution)/shard_map/ppermute | solution.py:35

commit v2 on v1

--- a/solution.py
+++ b/solution.py
@@ -43,12 +43,18 @@
     return slice(head * HD, (head + 1) * HD)
 
 
-def head_scores(query, keys, refkeys, bias, some):
+def head_scores(query, keys, refkeys, bias, some, turned=False):
     scores = {}
     for h in some:
         columns = head_columns(h)
         scores[h, 0] = dot_t(query[:, columns], keys[:, columns])
-        scores[h, 1] = dot_t(query[:, columns], refkeys[:, columns]) + bias
+        if turned:
+            found = jnp.dot(
+                query[:, columns], refkeys[columns, :], preferred_element_type=jnp.float32
+            )
+        else:
+            found = dot_t(query[:, columns], refkeys[:, columns])
+        scores[h, 1] = found + bias
     return scores
 
 
@@ -111,16 +117,18 @@
 
 
 def load_kernel(heads, ref_len, step_index, guide, *refs):
-    sources, w_ref, bias, scalars, targets, weight, w_here, sems = (
-        refs[:5], refs[5], refs[6], refs[7], refs[8:13], refs[13], refs[14], refs[15]
+    refk, sources, w_ref, bias, scalars, turned, targets, weight, w_here, refk_here, sems = (
+        refs[0], refs[1:5], refs[5], refs[6], refs[7], refs[8], refs[9:13], *refs[13:]
     )
     copies = [
         pltpu.make_async_copy(source, target, sems.at[i])
-        for i, (source, target) in enumerate(zip((w_ref, *sources), (w_here, *targets)))
+        for i, (source, target) in enumerate(
+            zip((w_ref, refk, *sources), (w_here, refk_here, *targets))
+        )
     ]
     for copy in copies:
         copy.start()
-    valid = ref_len[0] - lax.axis_index("seq") * sources[3].shape[0]
+    valid = ref_len[0] - lax.axis_index("seq") * refk.shape[0]
     index = lax.broadcasted_iota(jnp.int32, bias.shape, 1)
     bias[...] = jnp.where(index < valid, 0.0, jnp.float32(NEG))
     sig_now = sigma_of(step_index[0])
@@ -129,20 +137,23 @@
         scalars[8 * i : 8 * i + 8, :] = jnp.full((8, 128), scalar, jnp.float32)
     copies[0].wait()
     fill_weight(weight, w_here, heads)
-    for copy in copies[1:]:
+    copies[1].wait()
+    for h in range(heads):
+        turned[head_columns(h), :] = jnp.transpose(refk_here[:, head_columns(h)])
+    for copy in copies[2:]:
         copy.wait()
 
 
 def score_rows(heads, query, keys, refk, bias, exps_out):
     rows = query.shape[0]
-    count, others = refk.shape[0], keys.shape[0]
+    count, others = refk.shape[1], keys.shape[0]
     span = count + 128
     lane = lax.broadcasted_iota(jnp.int32, (rows, 128), 1)
     top_columns = jnp.zeros((rows, 128), jnp.float32)
     sum_columns = jnp.ones((rows, 128), jnp.float32)
     for first in range(0, heads, 8):
         some = range(first, first + 8)
-        tops, exps, totals = head_exps(head_scores(query, keys, refk, bias[0:1], some))
+        tops, exps, totals = head_exps(head_scores(query, keys, refk, bias[0:1], some, True))
         for h in some:
             start = h * span
             exps_out[:, start : start + count] = exps[h, 1].astype(jnp.bfloat16)
@@ -220,7 +231,7 @@
 
 
 def combine_kernel(
-    heads, scalars, own, o1, o2, o3, top, early, late, b0, b1, b2, b3, given, velocity
+    heads, scalars, own, o1, o2, o3, top, early, late, mine, across, side, given, velocity
 ):
     rows = own.shape[0]
     count = rows // 2
@@ -251,12 +262,15 @@
     first = jnp.where(low, even, pltpu.roll(odd, 64, 1))
     second = jnp.where(low, pltpu.roll(even, 64, 1), odd)
     half = count // 2
+    size = half // 2
     blocks = first[:half], first[half:], second[:half], second[half:]
     cfg = lax.axis_index("cfg") == 0
-    size = half // 2
-    for i, (block, kept) in enumerate(zip(blocks, (b0, b1, b2, b3))):
-        kept[...] = jnp.where(cfg, block[:size], block[size:])
-        given[i * 16 : i * 16 + size, :] = jnp.where(cfg, block[size:], block[:size])
+    side[...] = jnp.where(cfg, blocks[1], blocks[3])
+    given[:half] = jnp.where(cfg, blocks[3], blocks[1])
+    for i, kept in ((0, mine), (2, across)):
+        kept[...] = jnp.where(cfg, blocks[i][:size], blocks[i][size:])
+        start = 24 + 8 * i
+        given[start : start + size] = jnp.where(cfg, blocks[i][size:], blocks[i][:size])
 
 
 def share_of(own, everyone):
@@ -269,13 +283,18 @@
     return jnp.exp2(own - top) * (1.0 / total)
 
 
-def join_kernel(taken, b0, b1, b2, b3, g0, g1, g2, g3):
-    for i, (block, out) in enumerate(((b0, g0), (b1, g1), (b2, g2), (b3, g3))):
-        out[...] = block[...] + taken[i * 16 : i * 16 + out.shape[0], :]
-
-
-def euler_kernel(scalars, latent, own, r1, r2, r3, latent_next, denoised):
-    guided = (own[...] + r1[...]) + (r2[...] + r3[...])
+def join_kernel(taken, mine, across, side, mine_out, across_out, side_out):
+    rows, size = side.shape[0], mine.shape[0]
+    side_out[...] = side[...] + taken[:rows]
+    mine_out[...] = mine[...] + taken[24 : 24 + size]
+    across_out[...] = across[...] + taken[40 : 40 + size]
+
+
+def euler_kernel(scalars, latent, mine, across, side, other, latent_next, denoised):
+    size = mine.shape[0]
+    sides = side[...] + other[...]
+    sides = jnp.where(lax.axis_index("cfg") == 0, sides[:size], sides[size:])
+    guided = (mine[...] + across[...]) + sides
     latent_next[...] = latent[...] + scalars[16:17, :] * guided
     denoised[...] = latent[...] - scalars[8:9, :] * guided
 
@@ -299,7 +318,7 @@
     heads = width // HD
     rows, others = 2 * count, refk.shape[0]
     f32, bf16 = jnp.float32, jnp.bfloat16
-    sources = (query, keys, values, refk, refv)
+    sources = (query, keys, values, refv)
     k_other = swap(keys, "blk", 1)
     v_other = swap(values, "blk", 1)
     far_in = exchange(query, "seq", [(1, 2), (2, 1)])
@@ -307,20 +326,25 @@
     far_out = exchange(query, "seq", [(0, 3), (3, 0)])
     mid_in = exchange(query, "seq", [(0, 2), (3, 1)])
     mid_out = exchange(far_in, "seq", [(2, 3), (1, 0)])
-    bias, scalars, query, keys, values, refk, refv, weight = pl.pallas_call(
+    bias, scalars, refk, query, keys, values, refv, weight = pl.pallas_call(
         partial(load_kernel, heads),
         in_specs=[SMEM] * 3 + [pl.BlockSpec(memory_space=pltpu.HBM)] * 6,
         out_specs=[VMEM] * 8,
         out_shape=[pltpu.VMEM((8, others), f32), pltpu.VMEM((24, 128), f32)]
+        + [pltpu.VMEM((width, others), bf16)]
         + [pltpu.VMEM(a.shape, a.dtype) for a in sources]
         + [pltpu.VMEM((128, 2 * width), bf16)],
-        scratch_shapes=[pltpu.VMEM(w_t.shape, w_t.dtype), pltpu.SemaphoreType.DMA((6,))],
-        compiler_params=pltpu.CompilerParams(vmem_limit_bytes=2 << 20),
+        scratch_shapes=[
+            pltpu.VMEM(w_t.shape, w_t.dtype),
+            pltpu.VMEM(refk.shape, refk.dtype),
+            pltpu.SemaphoreType.DMA((6,)),
+        ],
+        compiler_params=pltpu.CompilerParams(vmem_limit_bytes=6 << 20),
         cost_estimate=pl.CostEstimate(
             flops=10000000, bytes_accessed=4 * refk.size, transcendentals=0
         ),
         name="load",
-    )(ref_len, step_index, guide, *[in_hbm(a) for a in (*sources, w_t)])
+    )(ref_len, step_index, guide, *[in_hbm(a) for a in (refk, *sources, w_t)])
     exps_shape = pltpu.VMEM((rows, heads * (others + 128)), bf16)
     columns = pltpu.VMEM((rows, 128), f32)
     stacked = pltpu.VMEM((rows, width), bf16)
@@ -356,18 +380,21 @@
         (exps_m, exps_f, values, refv, weight), [partial_shape], [exps_shape], flops=flops,
     )
     half = pltpu.VMEM(latent.shape, f32)
+    whole = pltpu.VMEM((count // 2, 128), f32)
     *kept, given = call(
         partial(combine_kernel, heads),
         (scalars, lse, o1, o2, o3, top, early, late),
-        [half] * 4 + [pltpu.VMEM((64, 128), f32)], [columns],
+        [half, half, whole, pltpu.VMEM((56, 128), f32)], [columns],
     )
     taken = swap(given, "cfg", 1)
-    blocks = call(join_kernel, (taken, *kept), [half] * 4, mib=2)
-    r3 = swap(blocks[3], "seq", 3)
-    r2 = swap(blocks[2], "seq", 2)
-    r1 = swap(blocks[1], "seq", 1)
+    mine, across, side = call(join_kernel, (taken, *kept), [half, half, whole], mib=2)
+    pairs = [(2 * z, 2 * (z ^ 1)) for z in range(4)]
+    pairs += [(2 * z + 1, 2 * (z ^ 3) + 1) for z in range(4)]
+    side = exchange(side, ("seq", "cfg"), pairs)
+    across = swap(across, "seq", 2)
+    other = swap(side, "cfg", 1)
     result = jax.ShapeDtypeStruct(latent.shape, latent.dtype)
-    return call(euler_kernel, (scalars, latent, blocks[0], r1, r2, r3), [result] * 2, mib=2)
+    return call(euler_kernel, (scalars, latent, mine, across, side, other), [result] * 2, mib=2)
 
 
 def attend_kernel(heads, valid, query, keys, values, refk, refv, w_ref, out, lse, share, weight):

time: 49.9 us -> 51.4 us (1.030)
  waiting for transfers between devices: 11.2 us -> 16.8 us
  starting transfers between devices: 24.3 us -> 20.8 us
    ppermute x14, waiting for transfers between devices: 11.2 us -> 16.8 us  [exchange(): return lax.ppermute(value, axis, pairs)]
    ppermute x14, starting transfers between devices: 24.3 us -> 20.8 us  [exchange(): return lax.ppermute(value, axis, pairs)]
  transfers between devices with their start and end apart: 14 -> 14, of which waited for: 8 -> 8; matrix products, arithmetic and copies ran while one was open for 0% -> 0% of each run, Pallas kernels for 20% -> 19%
where the time goes in v2:
time: 51.4 us; the launch traced here: 51.2 us
  starting transfers between devices  20.8 us (40%)
  waiting for transfers between devices  16.8 us (33%)
  Pallas kernels  11 us (21%)
  between operations  2.7 us (5%)
    ppermute x14, starting transfers between devices, exchange(): return lax.ppermute(value, axis, pairs)  20.8 us
    ppermute x14, waiting for transfers between devices, exchange(): return lax.ppermute(value, axis, pairs)  16.8 us
    pallas_call x8, Pallas kernels, call(): pl.pallas_call(kernel, in_specs=[VMEM] * len(arrays), out_specs=[VMEM] *...  8.19 us
    pallas_call x1, Pallas kernels, line_of_four(): pl.pallas_call(partial(load_kernel, heads), in_specs=[SMEM] * 3 + [pl.Blo...  2.77 us
  transfers between devices with their start and end apart: 14, of which 8 were waited for; matrix products, arithmetic and copies ran while one was open for 0% of the time, Pallas kernels for 19%

profile of v2, /device:TPU:0, one launch (start us, length us, event | category | flops | bytes accessed | tf_op | source)
XLA Modules:
  0.0 51.2 jit_solution(13394745726988550250)
XLA Ops:
  0.6 0.7 %collective-permute-start.1 = (bf16[40,4096]{1,0:T(8,128)(2,1)}, bf16[40,4096]{1,0:T(8,128)(2,1)S(1)}, u32[]{:S(2)}, u32[]{:S(2)}) collective-permute-start(bf16[40,4096]{1,0:T(8,128)(2,1)} %bitcast.11), channel_id=1, source_target_pairs={{4,8},{8,4},{5,9},{9,5},{6,10},{10,6},{7,11},{11,7},{20,24},{24,20... | collective-permute-start | bytes 983048 | tf_op jit(solution)/shard_map/ppermute | solution.py:35
  1.3 5.9 %collective-permute-start.3 = (bf16[40,4096]{1,0:T(8,128)(2,1)}, bf16[40,4096]{1,0:T(8,128)(2,1)S(1)}, u32[]{:S(2)}, u32[]{:S(2)}) collective-permute-start(bf16[40,4096]{1,0:T(8,128)(2,1)} %bitcast.12), channel_id=1, source_target_pairs={{0,4},{4,0},{8,12},{12,8},{1,5},{5,1},{9,13},{13,9},{2,6},{6,2},{1... | collective-permute-start | bytes 983048 | tf_op jit(solution)/shard_map/ppermute | solution.py:35
  7.2 1.5 %collective-permute-start.4 = (bf16[40,4096]{1,0:T(8,128)(2,1)}, bf16[40,4096]{1,0:T(8,128)(2,1)S(1)}, u32[]{:S(2)}, u32[]{:S(2)}) collective-permute-start(bf16[40,4096]{1,0:T(8,128)(2,1)} %bitcast.9), channel_id=1, source_target_pairs={{0,2},{2,0},{1,3},{3,1},{4,6},{6,4},{5,7},{7,5},{8,10},{10,8},{9,1... | collective-permute-start | bytes 983048 | tf_op jit(solution)/shard_map/ppermute | solution.py:35
  8.7 3.2 %collective-permute-start.5 = (bf16[40,4096]{1,0:T(8,128)(2,1)}, bf16[40,4096]{1,0:T(8,128)(2,1)S(1)}, u32[]{:S(2)}, u32[]{:S(2)}) collective-permute-start(bf16[40,4096]{1,0:T(8,128)(2,1)} %bitcast.13), channel_id=1, source_target_pairs={{0,12},{12,0},{1,13},{13,1},{2,14},{14,2},{3,15},{15,3},{16,28},{2... | collective-permute-start | bytes 983048 | tf_op jit(solution)/shard_map/ppermute | solution.py:35
  12.0 1.3 %collective-permute-start = (bf16[40,4096]{1,0:T(8,128)(2,1)}, bf16[40,4096]{1,0:T(8,128)(2,1)S(1)}, u32[]{:S(2)}, u32[]{:S(2)}) collective-permute-start(bf16[40,4096]{1,0:T(8,128)(2,1)} %bitcast.14), channel_id=1, source_target_pairs={{0,8},{12,4},{1,9},{13,5},{2,10},{14,6},{3,11},{15,7},{16,24},{28,... | collective-permute-start | bytes 983048 | tf_op jit(solution)/shard_map/ppermute | solution.py:35
  13.3 1.3 %collective-permute-start.2 = (bf16[40,4096]{1,0:T(8,128)(2,1)S(1)}, bf16[40,4096]{1,0:T(8,128)(2,1)S(1)}, u32[]{:S(2)}, u32[]{:S(2)}) collective-permute-start(bf16[40,4096]{1,0:T(8,128)(2,1)S(1)} %collective-permute-done.1.far_in), channel_id=1, source_target_pairs={{8,12},{4,0},{9,13},{5,1},{10,14},{6,2},{11,15},{7,3},{24,28},{20,... | collective-permute-start | bytes 983048 | tf_op jit(solution)/shard_map/ppermute | solution.py:35
  14.6 1.0 %collective-permute-done.3.near = bf16[40,4096]{1,0:T(8,128)(2,1)S(1)} collective-permute-done((bf16[40,4096]{1,0:T(8,128)(2,1)}, bf16[40,4096]{1,0:T(8,128)(2,1)S(1)}, u32[]{:S(2)}, u32[]{:S(2)}) %collective-permute-start.3) | collective-permute-done | bytes 327712 | tf_op jit(solution)/shard_map/ppermute | solution.py:35
  15.7 1.5 %collective-permute-start.9 = (bf16[40,4096]{1,0:T(8,128)(2,1)}, bf16[40,4096]{1,0:T(8,128)(2,1)S(1)}, u32[]{:S(2)}, u32[]{:S(2)}) collective-permute-start(bf16[40,4096]{1,0:T(8,128)(2,1)} %bitcast.16), channel_id=1, source_target_pairs={{0,2},{2,0},{1,3},{3,1},{4,6},{6,4},{5,7},{7,5},{8,10},{10,8},{9,1... | collective-permute-start | bytes 983048 | tf_op jit(solution)/shard_map/ppermute | solution.py:35
  19.1 2.8 %load.1 = (f32[8,256]{1,0:T(8,128)S(1)}, f32[24,128]{1,0:T(8,128)S(1)}, bf16[4096,256]{1,0:T(8,128)(2,1)S(1)}, bf16[40,4096]{1,0:T(8,128)(2,1)S(1)}, bf16[40,409...) custom-call(s32[1]{0:T(128)S(6)} %copy.12.ref_len, ...), custom_call_target="tpu_custom_call" | custom-call | flops 10000000 | bytes 4194304 | tf_op jit(solution)/shard_map/load/pallas_call | solution.py:329
  21.9 1.9 %shard_map.113 = (bf16[80,12288]{1,0:T(8,128)(2,1)S(1)}, f32[80,128]{1,0:T(8,128)S(1)}, f32[80,128]{1,0:T(8,128)S(1)}, bf16[80,4096]{1,0:T(8,128)(2,1)S(1)}) custom-call(bf16[40,4096]{1,0:T(8,128)(2,1)S(1)} %get-tuple-element.30.own, bf16[40,4096]{1,0:T(8,128)(2,1)S(1)} %collective-permute-done.3.near, bf16[40,4096]{1,0:T(8,128)(2,1)S(1)} %get-tuple-element.31.k0, ...), custom_call_target="tpu_custom_call" | custom-call | flops 220200960 | tf_op jit(solution)/shard_map/pallas_call | solution.py:303
  24.4 1.0 %shard_map.114 = (bf16[40,12288]{1,0:T(8,128)(2,1)S(1)}, f32[40,128]{1,0:T(8,128)S(1)}, f32[40,128]{1,0:T(8,128)S(1)}) custom-call(bf16[40,4096]{1,0:T(8,128)(2,1)S(1)} %collective-permute-done.1.far_in, bf16[40,4096]{1,0:T(8,128)(2,1)S(1)} %collective-permute-done.5.far_out, bf16[80,4096]{1,0:T(8,128)(2,1)S(1)} %get-tuple-element.34.keys, ...), custom_call_target="tpu_custom_call" | custom-call | flops 110100480 | tf_op jit(solution)/shard_map/pallas_call | solution.py:303
  25.4 2.9 %collective-permute-done.mid_in = bf16[40,4096]{1,0:T(8,128)(2,1)S(1)} collective-permute-done((bf16[40,4096]{1,0:T(8,128)(2,1)}, bf16[40,4096]{1,0:T(8,128)(2,1)S(1)}, u32[]{:S(2)}, u32[]{:S(2)}) %collective-permute-start) | collective-permute-done | bytes 327712 | tf_op jit(solution)/shard_map/ppermute | solution.py:35
  28.3 1.3 %collective-permute-done.2.mid_out = bf16[40,4096]{1,0:T(8,128)(2,1)S(1)} collective-permute-done((bf16[40,4096]{1,0:T(8,128)(2,1)S(1)}, bf16[40,4096]{1,0:T(8,128)(2,1)S(1)}, u32[]{:S(2)}, u32[]{:S(2)}) %collective-permute-start.2) | collective-permute-done | bytes 327712 | tf_op jit(solution)/shard_map/ppermute | solution.py:35
  29.6 1.1 %shard_map.115 = (bf16[40,12288]{1,0:T(8,128)(2,1)S(1)}, f32[80,128]{1,0:T(8,128)S(1)}, f32[80,128]{1,0:T(8,128)S(1)}) custom-call(bf16[40,4096]{1,0:T(8,128)(2,1)S(1)} %collective-permute-done.mid_in, bf16[40,4096]{1,0:T(8,128)(2,1)S(1)} %collective-permute-done.2.mid_out, bf16[80,4096]{1,0:T(8,128)(2,1)S(1)} %get-tuple-element.34.keys, ...), custom_call_target="tpu_custom_call" | custom-call | flops 110100480 | tf_op jit(solution)/shard_map/pallas_call | solution.py:303
  30.7 1.1 %collective-permute-start.6 = (f32[80,128]{1,0:T(8,128)S(1)}, f32[80,128]{1,0:T(8,128)S(1)}, u32[]{:S(2)}, u32[]{:S(2)}) collective-permute-start(f32[80,128]{1,0:T(8,128)S(1)} %get-tuple-element.39.own), channel_id=1, source_target_pairs={{0,4},{4,0},{8,12},{12,8},{1,5},{5,1},{9,13},{13,9},{2,6},{6,2},{1... | collective-permute-start | bytes 122888 | tf_op jit(solution)/shard_map/ppermute | solution.py:35
  31.7 2.0 %collective-permute-start.7 = (f32[80,128]{1,0:T(8,128)S(1)}, f32[80,128]{1,0:T(8,128)S(1)}, u32[]{:S(2)}, u32[]{:S(2)}) collective-permute-start(f32[80,128]{1,0:T(8,128)S(1)} %get-tuple-element.39.own), channel_id=1, source_target_pairs={{0,8},{4,12},{8,0},{12,4},{1,9},{5,13},{9,1},{13,5},{2,10},{6,14},... | collective-permute-start | bytes 122888 | tf_op jit(solution)/shard_map/ppermute | solution.py:35
  33.8 1.3 %collective-permute-start.8 = (f32[80,128]{1,0:T(8,128)S(1)}, f32[80,128]{1,0:T(8,128)S(1)}, u32[]{:S(2)}, u32[]{:S(2)}) collective-permute-start(f32[80,128]{1,0:T(8,128)S(1)} %get-tuple-element.39.own), channel_id=1, source_target_pairs={{0,12},{4,8},{8,4},{12,0},{1,13},{5,9},{9,5},{13,1},{2,14},{6,10},... | collective-permute-start | bytes 122888 | tf_op jit(solution)/shard_map/ppermute | solution.py:35
  35.1 1.5 %shard_map.116 = (f32[4096,80]{1,0:T(8,128)S(1)}, bf16[80,4096]{1,0:T(8,128)(2,1)S(1)}) custom-call(bf16[80,12288]{1,0:T(8,128)(2,1)S(1)} %get-tuple-element.41.exps, bf16[40,4096]{1,0:T(8,128)(2,1)S(1)} %get-tuple-element.42.v0, bf16[40,4096]{1,0:T(8,128)(2,1)S(1)} %collective-permute-done.9.v1, bf16[256,4096]{1,0:T(8,128)(2,1)S(1)} %get-tuple-element.43.refv, ...), custom_call_target="tpu_custom_call" | custom-call | flops 220200960 | tf_op jit(solution)/shard_map/pallas_call | solution.py:303
  36.6 1.4 %shard_map.117.late = f32[4096,80]{1,0:T(8,128)S(1)} custom-call(bf16[40,12288]{1,0:T(8,128)(2,1)S(1)} %get-tuple-element.46.middle, bf16[40,12288]{1,0:T(8,128)(2,1)S(1)} %get-tuple-element.47.far, bf16[80,4096]{1,0:T(8,128)(2,1)S(1)} %get-tuple-element.48.values, bf16[256,4096]{1,0:T(8,128)(2,1)S(1)} %get-tuple-element.43.refv, ...), custom_call_target="tpu_custom_call" | custom-call | flops 220200960 | tf_op jit(solution)/shard_map/pallas_call | solution.py:303
  38.0 1.6 %collective-permute-done.8.o3 = f32[80,128]{1,0:T(8,128)S(1)} collective-permute-done((f32[80,128]{1,0:T(8,128)S(1)}, f32[80,128]{1,0:T(8,128)S(1)}, u32[]{:S(2)}, u32[]{:S(2)}) %collective-permute-start.8) | collective-permute-done | bytes 40992 | tf_op jit(solution)/shard_map/ppermute | solution.py:35
  40.3 1.2 %collective-permute-done.10.taken = f32[56,128]{1,0:T(8,128)S(1)} collective-permute-done((f32[56,128]{1,0:T(8,128)S(1)}, f32[56,128]{1,0:T(8,128)S(1)}, u32[]{:S(2)}, u32[]{:S(2)}) %collective-permute-start.10) | collective-permute-done | bytes 28704 | tf_op jit(solution)/shard_map/ppermute | solution.py:35
  41.5 3.7 %collective-permute-done.12.side = f32[20,128]{1,0:T(8,128)S(1)} collective-permute-done((f32[20,128]{1,0:T(8,128)S(1)}, f32[20,128]{1,0:T(8,128)S(1)}, u32[]{:S(2)}, u32[]{:S(2)}) %collective-permute-start.12) | collective-permute-done | bytes 10272 | tf_op jit(solution)/shard_map/ppermute | solution.py:35
  45.2 0.8 %collective-permute-start.13 = (f32[20,128]{1,0:T(8,128)S(1)}, f32[20,128]{1,0:T(8,128)S(1)}, u32[]{:S(2)}, u32[]{:S(2)}) collective-permute-start(f32[20,128]{1,0:T(8,128)S(1)} %collective-permute-done.12.side), channel_id=1, source_target_pairs={{0,1},{1,0},{2,3},{3,2},{4,5},{5,4},{6,7},{7,6},{8,9},{9,8},{10,11... | collective-permute-start | bytes 30728 | tf_op jit(solution)/shard_map/ppermute | solution.py:35
  46.1 4.5 %collective-permute-done.11.across = f32[10,128]{1,0:T(8,128)S(1)} collective-permute-done((f32[10,128]{1,0:T(8,128)S(1)}, f32[10,128]{1,0:T(8,128)S(1)}, u32[]{:S(2)}, u32[]{:S(2)}) %collective-permute-start.11) | collective-permute-done | bytes 5152 | tf_op jit(solution)/shard_map/ppermute | solution.py:35
  (15 shorter events, 2.0 us)
Async XLA Ops:
  0.6 12.7 %collective-permute-start.1 = (bf16[40,4096]{1,0:T(8,128)(2,1)}, bf16[40,4096]{1,0:T(8,128)(2,1)S(1)}, u32[]{:S(2)}, u32[]{:S(2)}) collective-permute-start(bf16[40,4096]{1,0:T(8,128)(2,1)} %bitcast.11), channel_id=1, source_target_pairs={{4,8},{8,4},{5,9},{9,5},{6,10},{10,6},{7,11},{11,7},{20,24},{24,20... | collective-permute-start | bytes 983048 | tf_op jit(solution)/shard_map/ppermute | solution.py:35
  1.3 14.3 %collective-permute-start.3 = (bf16[40,4096]{1,0:T(8,128)(2,1)}, bf16[40,4096]{1,0:T(8,128)(2,1)S(1)}, u32[]{:S(2)}, u32[]{:S(2)}) collective-permute-start(bf16[40,4096]{1,0:T(8,128)(2,1)} %bitcast.12), channel_id=1, source_target_pairs={{0,4},{4,0},{8,12},{12,8},{1,5},{5,1},{9,13},{13,9},{2,6},{6,2},{1... | collective-permute-start | bytes 983048 | tf_op jit(solution)/shard_map/ppermute | solution.py:35
  7.2 14.6 %collective-permute-start.4 = (bf16[40,4096]{1,0:T(8,128)(2,1)}, bf16[40,4096]{1,0:T(8,128)(2,1)S(1)}, u32[]{:S(2)}, u32[]{:S(2)}) collective-permute-start(bf16[40,4096]{1,0:T(8,128)(2,1)} %bitcast.9), channel_id=1, source_target_pairs={{0,2},{2,0},{1,3},{3,1},{4,6},{6,4},{5,7},{7,5},{8,10},{10,8},{9,1... | collective-permute-start | bytes 983048 | tf_op jit(solution)/shard_map/ppermute | solution.py:35
  8.7 15.6 %collective-permute-start.5 = (bf16[40,4096]{1,0:T(8,128)(2,1)}, bf16[40,4096]{1,0:T(8,128)(2,1)S(1)}, u32[]{:S(2)}, u32[]{:S(2)}) collective-permute-start(bf16[40,4096]{1,0:T(8,128)(2,1)} %bitcast.13), channel_id=1, source_target_pairs={{0,12},{12,0},{1,13},{13,1},{2,14},{14,2},{3,15},{15,3},{16,28},{2... | collective-permute-start | bytes 983048 | tf_op jit(solution)/shard_map/ppermute | solution.py:35
  12.0 16.3 %collective-permute-start = (bf16[40,4096]{1,0:T(8,128)(2,1)}, bf16[40,4096]{1,0:T(8,128)(2,1)S(1)}, u32[]{:S(2)}, u32[]{:S(2)}) collective-permute-start(bf16[40,4096]{1,0:T(8,128)(2,1)} %bitcast.14), channel_id=1, source_target_pairs={{0,8},{12,4},{1,9},{13,5},{2,10},{14,6},{3,11},{15,7},{16,24},{28,... | collective-permute-start | bytes 983048 | tf_op jit(solution)/shard_map/ppermute | solution.py:35
  13.3 16.3 %collective-permute-start.2 = (bf16[40,4096]{1,0:T(8,128)(2,1)S(1)}, bf16[40,4096]{1,0:T(8,128)(2,1)S(1)}, u32[]{:S(2)}, u32[]{:S(2)}) collective-permute-start(bf16[40,4096]{1,0:T(8,128)(2,1)S(1)} %collective-permute-done.1.far_in), channel_id=1, source_target_pairs={{8,12},{4,0},{9,13},{5,1},{10,14},{6,2},{11,15},{7,3},{24,28},{20,... | collective-permute-start | bytes 983048 | tf_op jit(solution)/shard_map/ppermute | solution.py:35
  15.7 19.5 %collective-permute-start.9 = (bf16[40,4096]{1,0:T(8,128)(2,1)}, bf16[40,4096]{1,0:T(8,128)(2,1)S(1)}, u32[]{:S(2)}, u32[]{:S(2)}) collective-permute-start(bf16[40,4096]{1,0:T(8,128)(2,1)} %bitcast.16), channel_id=1, source_target_pairs={{0,2},{2,0},{1,3},{3,1},{4,6},{6,4},{5,7},{7,5},{8,10},{10,8},{9,1... | collective-permute-start | bytes 983048 | tf_op jit(solution)/shard_map/ppermute | solution.py:35
  30.7 7.3 %collective-permute-start.6 = (f32[80,128]{1,0:T(8,128)S(1)}, f32[80,128]{1,0:T(8,128)S(1)}, u32[]{:S(2)}, u32[]{:S(2)}) collective-permute-start(f32[80,128]{1,0:T(8,128)S(1)} %get-tuple-element.39.own), channel_id=1, source_target_pairs={{0,4},{4,0},{8,12},{12,8},{1,5},{5,1},{9,13},{13,9},{2,6},{6,2},{1... | collective-permute-start | bytes 122888 | tf_op jit(solution)/shard_map/ppermute | solution.py:35
  31.7 6.3 %collective-permute-start.7 = (f32[80,128]{1,0:T(8,128)S(1)}, f32[80,128]{1,0:T(8,128)S(1)}, u32[]{:S(2)}, u32[]{:S(2)}) collective-permute-start(f32[80,128]{1,0:T(8,128)S(1)} %get-tuple-element.39.own), channel_id=1, source_target_pairs={{0,8},{4,12},{8,0},{12,4},{1,9},{5,13},{9,1},{13,5},{2,10},{6,14},... | collective-permute-start | bytes 122888 | tf_op jit(solution)/shard_map/ppermute | solution.py:35
  33.8 5.8 %collective-permute-start.8 = (f32[80,128]{1,0:T(8,128)S(1)}, f32[80,128]{1,0:T(8,128)S(1)}, u32[]{:S(2)}, u32[]{:S(2)}) collective-permute-start(f32[80,128]{1,0:T(8,128)S(1)} %get-tuple-element.39.own), channel_id=1, source_target_pairs={{0,12},{4,8},{8,4},{12,0},{1,13},{5,9},{9,5},{13,1},{2,14},{6,10},... | collective-permute-start | bytes 122888 | tf_op jit(solution)/shard_map/ppermute | solution.py:35
  39.6 11.0 %copy-start = (f32[10,128]{1,0:T(8,128)S(1)}, f32[10,128]{1,0:T(8,128)}, u32[]{:S(2)}) copy-start(f32[10,128]{1,0:T(8,128)} %latent.1) | copy-start | bytes 15364
  40.3 1.3 %collective-permute-start.10 = (f32[56,128]{1,0:T(8,128)S(1)}, f32[56,128]{1,0:T(8,128)S(1)}, u32[]{:S(2)}, u32[]{:S(2)}) collective-permute-start(f32[56,128]{1,0:T(8,128)S(1)} %get-tuple-element.49), channel_id=1, source_target_pairs={{0,1},{1,0},{2,3},{3,2},{4,5},{5,4},{6,7},{7,6},{8,9},{9,8},{10,11... | collective-permute-start | bytes 86024 | tf_op jit(solution)/shard_map/ppermute | solution.py:35
  41.5 3.7 %collective-permute-start.12 = (f32[20,128]{1,0:T(8,128)S(1)}, f32[20,128]{1,0:T(8,128)S(1)}, u32[]{:S(2)}, u32[]{:S(2)}) collective-permute-start(f32[20,128]{1,0:T(8,128)S(1)} %get-tuple-element.55), channel_id=1, source_target_pairs={{0,4},{4,0},{8,12},{12,8},{1,13},{5,9},{9,5},{13,1},{2,6},{6,2},{1... | collective-permute-start | bytes 30728 | tf_op jit(solution)/shard_map/ppermute | solution.py:35
  45.2 5.4 %collective-permute-start.13 = (f32[20,128]{1,0:T(8,128)S(1)}, f32[20,128]{1,0:T(8,128)S(1)}, u32[]{:S(2)}, u32[]{:S(2)}) collective-permute-start(f32[20,128]{1,0:T(8,128)S(1)} %collective-permute-done.12.side), channel_id=1, source_target_pairs={{0,1},{1,0},{2,3},{3,2},{4,5},{5,4},{6,7},{7,6},{8,9},{9,8},{10,11... | collective-permute-start | bytes 30728 | tf_op jit(solution)/shard_map/ppermute | solution.py:35
  46.0 4.5 %collective-permute-start.11 = (f32[10,128]{1,0:T(8,128)S(1)}, f32[10,128]{1,0:T(8,128)S(1)}, u32[]{:S(2)}, u32[]{:S(2)}) collective-permute-start(f32[10,128]{1,0:T(8,128)S(1)} %get-tuple-element.54), channel_id=1, source_target_pairs={{0,8},{4,12},{8,0},{12,4},{1,9},{5,13},{9,1},{13,5},{2,10},{6,14},... | collective-permute-start | bytes 15368 | tf_op jit(solution)/shard_map/ppermute | solution.py:35

commit v3 on v2

--- a/solution.py
+++ b/solution.py
@@ -43,17 +43,16 @@
     return slice(head * HD, (head + 1) * HD)
 
 
-def head_scores(query, keys, refkeys, bias, some, turned=False):
+def head_scores(query, keys, refkeys, bias, some, base=0, turned=False):
     scores = {}
     for h in some:
         columns = head_columns(h)
-        scores[h, 0] = dot_t(query[:, columns], keys[:, columns])
+        here = query[:, head_columns(h - base)]
+        scores[h, 0] = dot_t(here, keys[:, columns])
         if turned:
-            found = jnp.dot(
-                query[:, columns], refkeys[columns, :], preferred_element_type=jnp.float32
-            )
+            found = jnp.dot(here, refkeys[columns, :], preferred_element_type=jnp.float32)
         else:
-            found = dot_t(query[:, columns], refkeys[:, columns])
+            found = dot_t(here, refkeys[:, columns])
         scores[h, 1] = found + bias
     return scores
 
@@ -144,18 +143,19 @@
         copy.wait()
 
 
-def score_rows(heads, query, keys, refk, bias, exps_out):
+def score_rows(heads, query, keys, refk, bias, exps_out, base=0):
     rows = query.shape[0]
     count, others = refk.shape[1], keys.shape[0]
     span = count + 128
     lane = lax.broadcasted_iota(jnp.int32, (rows, 128), 1)
     top_columns = jnp.zeros((rows, 128), jnp.float32)
     sum_columns = jnp.ones((rows, 128), jnp.float32)
-    for first in range(0, heads, 8):
+    for first in range(base, base + heads, 8):
         some = range(first, first + 8)
-        tops, exps, totals = head_exps(head_scores(query, keys, refk, bias[0:1], some, True))
+        scores = head_scores(query, keys, refk, bias[0:1], some, base, True)
+        tops, exps, totals = head_exps(scores)
         for h in some:
-            start = h * span
+            start = (h - base) * span
             exps_out[:, start : start + count] = exps[h, 1].astype(jnp.bfloat16)
             start += count
             exps_out[:, start : start + others] = exps[h, 0].astype(jnp.bfloat16)
@@ -203,10 +203,25 @@
     lse[...], top[...] = score_rows(heads, query, keys, refk, bias, exps)
 
 
-def middle_scores_kernel(
-    heads, mid_in, mid_out, keys, refk, bias, lse_early, top_early, lse_far, top_far,
-    exps, lse, top, query,
-):
+def cut_kernel(source, left, right):
+    half = left.shape[1]
+    left[...] = source[:, :half]
+    right[...] = source[:, half:]
+
+
+def cut_hbm_kernel(source, left, right, sems):
+    half = left.shape[1]
+    copies = [
+        pltpu.make_async_copy(source.at[:, pl.ds(i * half, out.shape[1])], out, sems.at[i])
+        for i, out in enumerate((left, right))
+    ]
+    for copy in copies:
+        copy.start()
+    for copy in copies:
+        copy.wait()
+
+
+def fill_middle(query, mid_in, mid_out):
     @pl.when(is_inner())
     def _():
         query[...] = mid_in[...]
@@ -215,18 +230,37 @@
     def _():
         query[...] = mid_out[...]
 
+
+def middle_first_kernel(heads, mid_in, mid_out, keys, refk, bias, exps, lse, top, query):
+    fill_middle(query, mid_in, mid_out)
+    lse[...], top[...] = score_rows(heads, query, keys, refk, bias, exps)
+
+
+def middle_second_kernel(
+    base, heads, mid_in, mid_out, keys, refk, bias, lse_early, top_early, lse_far, top_far,
+    lse_first, top_first, exps, lse, top, query,
+):
+    fill_middle(query, mid_in, mid_out)
     count = query.shape[0]
-    low = lax.broadcasted_iota(jnp.int32, (count, 128), 1) < 64
+    lane = lax.broadcasted_iota(jnp.int32, (count, 128), 1)
+    low = lane < 64
     far_lse, far_top = pltpu.roll(lse_far[...], 64, 1), pltpu.roll(top_far[...], 64, 1)
     lse[count:] = jnp.where(low, lse_early[count:], far_lse)
     top[count:] = jnp.where(low, top_early[count:], far_top)
-    found = score_rows(heads, query, keys, refk, bias, exps)
-    lse[:count] = jnp.where(low, lse_early[:count], pltpu.roll(found[0], 64, 1))
-    top[:count] = jnp.where(low, top_early[:count], pltpu.roll(found[1], 64, 1))
-
-
-def late_values_kernel(heads, middle, far, values, refv, weight, out, exps):
-    fill_rows(exps, (middle, far))
+    found = score_rows(heads, query, keys, refk, bias, exps, base)
+    before = lane % 32 < base
+    for out, early, first, second in (
+        (lse, lse_early, lse_first, found[0]), (top, top_early, top_first, found[1]),
+    ):
+        both = jnp.where(before, first[...], second)
+        out[:count] = jnp.where(low, early[:count], pltpu.roll(both, 64, 1))
+
+
+def late_values_kernel(heads, first, second, far, values, refv, weight, out, exps):
+    count, half = first.shape
+    exps[:count, :half] = first[...]
+    exps[:count, half:] = second[...]
+    exps[count:] = far[...]
     value_rows(heads, exps, values, refv, weight, out)
 
 
@@ -324,8 +358,25 @@
     far_in = exchange(query, "seq", [(1, 2), (2, 1)])
     near = swap(query, "seq", 1)
     far_out = exchange(query, "seq", [(0, 3), (3, 0)])
-    mid_in = exchange(query, "seq", [(0, 2), (3, 1)])
-    mid_out = exchange(far_in, "seq", [(2, 3), (1, 0)])
+    ahead = heads - heads // 4
+    part_shapes = [
+        pltpu.VMEM((count, ahead * HD), bf16),
+        pltpu.VMEM((count, width - ahead * HD), bf16),
+    ]
+    own_parts = pl.pallas_call(
+        cut_hbm_kernel,
+        in_specs=[pl.BlockSpec(memory_space=pltpu.HBM)],
+        out_specs=[VMEM] * 2,
+        out_shape=part_shapes,
+        scratch_shapes=[pltpu.SemaphoreType.DMA((2,))],
+        compiler_params=pltpu.CompilerParams(vmem_limit_bytes=2 << 20),
+        name="cut_own",
+    )(in_hbm(query))
+    mid_in_first = exchange(own_parts[0], "seq", [(0, 2), (3, 1)])
+    mid_in_second = exchange(own_parts[1], "seq", [(0, 2), (3, 1)])
+    far_parts = call(cut_kernel, (far_in,), part_shapes, mib=2)
+    mid_out_first = exchange(far_parts[0], "seq", [(2, 3), (1, 0)])
+    mid_out_second = exchange(far_parts[1], "seq", [(2, 3), (1, 0)])
     bias, scalars, refk, query, keys, values, refv, weight = pl.pallas_call(
         partial(load_kernel, heads),
         in_specs=[SMEM] * 3 + [pl.BlockSpec(memory_space=pltpu.HBM)] * 6,
@@ -367,17 +418,27 @@
         (far_in, far_out, keys, refk, bias),
         [small, column, column], [block_shape], flops=flops // 2,
     )
-    exps_m, lse, top = call(
-        partial(middle_scores_kernel, heads),
-        (mid_in, mid_out, keys, refk, bias, lse_e, top_e, lse_f, top_f),
-        [small, columns, columns], [block_shape], flops=flops // 2,
+    cuts = [pltpu.VMEM((count, n * (others + 128)), bf16) for n in (ahead, heads - ahead)]
+    exps_m, lse_m, top_m = call(
+        partial(middle_first_kernel, ahead),
+        (mid_in_first, mid_out_first, keys, refk, bias),
+        [cuts[0], column, column], part_shapes[:1], flops=flops // 4,
+    )
+    exps_n, lse, top = call(
+        partial(middle_second_kernel, ahead, heads - ahead),
+        (
+            mid_in_second, mid_out_second, keys, refk, bias,
+            lse_e, top_e, lse_f, top_f, lse_m, top_m,
+        ),
+        [cuts[1], columns, columns], part_shapes[1:], flops=flops // 4,
     )
     o3 = swap(lse, "seq", 3)
     o2 = swap(lse, "seq", 2)
     o1 = swap(lse, "seq", 1)
     (late,) = call(
         partial(late_values_kernel, heads),
-        (exps_m, exps_f, values, refv, weight), [partial_shape], [exps_shape], flops=flops,
+        (exps_m, exps_n, exps_f, values, refv, weight),
+        [partial_shape], [exps_shape], flops=flops,
     )
     half = pltpu.VMEM(latent.shape, f32)
     whole = pltpu.VMEM((count // 2, 128), f32)

time: 51.4 us -> 56.4 us (1.097)
  starting transfers between devices: 20.8 us -> 29.8 us
  waiting for transfers between devices: 16.8 us -> 11.1 us
  Pallas kernels: 11 us -> 12.3 us
    ppermute x14 -> x16, starting transfers between devices: 20.8 us -> 29.8 us  [exchange(): return lax.ppermute(value, axis, pairs)]
    ppermute x14 -> x16, waiting for transfers between devices: 16.8 us -> 11.1 us  [exchange(): return lax.ppermute(value, axis, pairs)]
    pallas_call x0 -> x1, Pallas kernels: none -> 1.03 us  [line_of_four(): pl.pallas_call(cut_hbm_kernel, in_specs=[pl.BlockSpec(memory_space=pltpu....]
    pallas_call x8 -> x10, Pallas kernels: 8.19 us -> 8.54 us  [call(): pl.pallas_call(kernel, in_specs=[VMEM] * len(arrays), out_specs=[VMEM] *...]
  transfers between devices with their start and end apart: 14 -> 16, of which waited for: 8 -> 5; matrix products, arithmetic and copies ran while one was open for 0% -> 0% of each run, Pallas kernels for 19% -> 20%
where the time goes in v3:
time: 56.4 us; the launch traced here: 56.1 us
  starting transfers between devices  29.8 us (53%)
  Pallas kernels  12.3 us (22%)
  waiting for transfers between devices  11.1 us (20%)
  between operations  2.77 us (5%)
    ppermute x16, starting transfers between devices, exchange(): return lax.ppermute(value, axis, pairs)  29.8 us
    ppermute x16, waiting for transfers between devices, exchange(): return lax.ppermute(value, axis, pairs)  11.1 us
    pallas_call x10, Pallas kernels, call(): pl.pallas_call(kernel, in_specs=[VMEM] * len(arrays), out_specs=[VMEM] *...  8.54 us
    pallas_call x1, Pallas kernels, line_of_four(): pl.pallas_call(partial(load_kernel, heads), in_specs=[SMEM] * 3 + [pl.Blo...  2.77 us
  transfers between devices with their start and end apart: 16, of which 5 were waited for; matrix products, arithmetic and copies ran while one was open for 0% of the time, Pallas kernels for 20%

profile of v3, /device:TPU:0, one launch (start us, length us, event | category | flops | bytes accessed | tf_op | source)
XLA Modules:
  0.0 56.1 jit_solution(11908214712207608118)
XLA Ops:
  0.6 0.7 %collective-permute-start.1 = (bf16[40,4096]{1,0:T(8,128)(2,1)}, bf16[40,4096]{1,0:T(8,128)(2,1)S(1)}, u32[]{:S(2)}, u32[]{:S(2)}) collective-permute-start(bf16[40,4096]{1,0:T(8,128)(2,1)} %bitcast.8), channel_id=1, source_target_pairs={{4,8},{8,4},{5,9},{9,5},{6,10},{10,6},{7,11},{11,7},{20,24},{24,20... | collective-permute-start | bytes 983048 | tf_op jit(solution)/shard_map/ppermute | solution.py:35
  1.3 5.9 %collective-permute-start.3 = (bf16[40,4096]{1,0:T(8,128)(2,1)}, bf16[40,4096]{1,0:T(8,128)(2,1)S(1)}, u32[]{:S(2)}, u32[]{:S(2)}) collective-permute-start(bf16[40,4096]{1,0:T(8,128)(2,1)} %bitcast.9), channel_id=1, source_target_pairs={{0,4},{4,0},{8,12},{12,8},{1,5},{5,1},{9,13},{13,9},{2,6},{6,2},{1... | collective-permute-start | bytes 983048 | tf_op jit(solution)/shard_map/ppermute | solution.py:35
  7.2 1.5 %collective-permute-start.4 = (bf16[40,4096]{1,0:T(8,128)(2,1)}, bf16[40,4096]{1,0:T(8,128)(2,1)S(1)}, u32[]{:S(2)}, u32[]{:S(2)}) collective-permute-start(bf16[40,4096]{1,0:T(8,128)(2,1)} %bitcast.14), channel_id=1, source_target_pairs={{0,2},{2,0},{1,3},{3,1},{4,6},{6,4},{5,7},{7,5},{8,10},{10,8},{9,1... | collective-permute-start | bytes 983048 | tf_op jit(solution)/shard_map/ppermute | solution.py:35
  8.7 3.2 %collective-permute-start.5 = (bf16[40,4096]{1,0:T(8,128)(2,1)}, bf16[40,4096]{1,0:T(8,128)(2,1)S(1)}, u32[]{:S(2)}, u32[]{:S(2)}) collective-permute-start(bf16[40,4096]{1,0:T(8,128)(2,1)} %bitcast.10), channel_id=1, source_target_pairs={{0,12},{12,0},{1,13},{13,1},{2,14},{14,2},{3,15},{15,3},{16,28},{2... | collective-permute-start | bytes 983048 | tf_op jit(solution)/shard_map/ppermute | solution.py:35
  12.6 1.0 %cut_own.1 = (bf16[40,3072]{1,0:T(8,128)(2,1)S(1)}, bf16[40,1024]{1,0:T(8,128)(2,1)S(1)}) custom-call(bf16[40,4096]{1,0:T(8,128)(2,1)} %bitcast.11), custom_call_target="tpu_custom_call" | custom-call | tf_op jit(solution)/shard_map/cut_own/pallas_call | solution.py:366
  13.6 4.7 %collective-permute-start.6 = (bf16[40,3072]{1,0:T(8,128)(2,1)S(1)}, bf16[40,3072]{1,0:T(8,128)(2,1)S(1)}, u32[]{:S(2)}, u32[]{:S(2)}) collective-permute-start(bf16[40,3072]{1,0:T(8,128)(2,1)S(1)} %get-tuple-element.48), channel_id=1, source_target_pairs={{0,8},{12,4},{1,9},{13,5},{2,10},{14,6},{3,11},{15,7},{16,24},{28,... | collective-permute-start | bytes 737288 | tf_op jit(solution)/shard_map/ppermute | solution.py:35
  18.3 1.3 %collective-permute-start.7 = (bf16[40,3072]{1,0:T(8,128)(2,1)S(1)}, bf16[40,3072]{1,0:T(8,128)(2,1)S(1)}, u32[]{:S(2)}, u32[]{:S(2)}) collective-permute-start(bf16[40,3072]{1,0:T(8,128)(2,1)S(1)} %get-tuple-element.49), channel_id=1, source_target_pairs={{8,12},{4,0},{9,13},{5,1},{10,14},{6,2},{11,15},{7,3},{24,28},{20,... | collective-permute-start | bytes 737288 | tf_op jit(solution)/shard_map/ppermute | solution.py:35
  19.7 4.4 %collective-permute-start = (bf16[40,1024]{1,0:T(8,128)(2,1)S(1)}, bf16[40,1024]{1,0:T(8,128)(2,1)S(1)}, u32[]{:S(2)}, u32[]{:S(2)}) collective-permute-start(bf16[40,1024]{1,0:T(8,128)(2,1)S(1)} %get-tuple-element.37), channel_id=1, source_target_pairs={{0,8},{12,4},{1,9},{13,5},{2,10},{14,6},{3,11},{15,7},{16,24},{28,... | collective-permute-start | bytes 245768 | tf_op jit(solution)/shard_map/ppermute | solution.py:35
  24.4 1.3 %collective-permute-start.2 = (bf16[40,1024]{1,0:T(8,128)(2,1)S(1)}, bf16[40,1024]{1,0:T(8,128)(2,1)S(1)}, u32[]{:S(2)}, u32[]{:S(2)}) collective-permute-start(bf16[40,1024]{1,0:T(8,128)(2,1)S(1)} %get-tuple-element.38), channel_id=1, source_target_pairs={{8,12},{4,0},{9,13},{5,1},{10,14},{6,2},{11,15},{7,3},{24,28},{20,... | collective-permute-start | bytes 245768 | tf_op jit(solution)/shard_map/ppermute | solution.py:35
  27.6 2.8 %load.1 = (f32[8,256]{1,0:T(8,128)S(1)}, f32[24,128]{1,0:T(8,128)S(1)}, bf16[4096,256]{1,0:T(8,128)(2,1)S(1)}, bf16[40,4096]{1,0:T(8,128)(2,1)S(1)}, bf16[40,409...) custom-call(s32[1]{0:T(128)S(6)} %copy.12.ref_len, ...), custom_call_target="tpu_custom_call" | custom-call | flops 10000000 | bytes 4194304 | tf_op jit(solution)/shard_map/load/pallas_call | solution.py:380
  30.4 1.9 %shard_map.114 = (bf16[80,12288]{1,0:T(8,128)(2,1)S(1)}, f32[80,128]{1,0:T(8,128)S(1)}, f32[80,128]{1,0:T(8,128)S(1)}, bf16[80,4096]{1,0:T(8,128)(2,1)S(1)}) custom-call(bf16[40,4096]{1,0:T(8,128)(2,1)S(1)} %get-tuple-element.39.own, bf16[40,4096]{1,0:T(8,128)(2,1)S(1)} %collective-permute-done.3.near, bf16[40,4096]{1,0:T(8,128)(2,1)S(1)} %get-tuple-element.40.k0, ...), custom_call_target="tpu_custom_call" | custom-call | flops 220200960 | tf_op jit(solution)/shard_map/pallas_call | solution.py:337
  32.3 1.1 %shard_map.115 = (bf16[40,12288]{1,0:T(8,128)(2,1)S(1)}, f32[40,128]{1,0:T(8,128)S(1)}, f32[40,128]{1,0:T(8,128)S(1)}) custom-call(bf16[40,4096]{1,0:T(8,128)(2,1)S(1)} %collective-permute-done.1.source.far_in, bf16[40,4096]{1,0:T(8,128)(2,1)S(1)} %collective-permute-done.5.far_out, bf16[80,4096]{1,0:T(8,128)(2,1)S(1)} %get-tuple-element.43.keys, ...), custom_call_target="tpu_custom_call" | custom-call | flops 110100480 | tf_op jit(solution)/shard_map/pallas_call | solution.py:337
  33.4 0.9 %shard_map.116 = (bf16[40,9216]{1,0:T(8,128)(2,1)S(1)}, f32[40,128]{1,0:T(8,128)S(1)}, f32[40,128]{1,0:T(8,128)S(1)}) custom-call(bf16[40,3072]{1,0:T(8,128)(2,1)S(1)} %collective-permute-done.6.mid_in, bf16[40,3072]{1,0:T(8,128)(2,1)S(1)} %collective-permute-done.7.mid_out, bf16[80,4096]{1,0:T(8,128)(2,1)S(1)} %get-tuple-element.43.keys, ...), custom_call_target="tpu_custom_call" | custom-call | flops 55050240 | tf_op jit(solution)/shard_map/pallas_call | solution.py:337
  34.8 2.7 %collective-permute-start.8 = (f32[80,128]{1,0:T(8,128)S(1)}, f32[80,128]{1,0:T(8,128)S(1)}, u32[]{:S(2)}, u32[]{:S(2)}) collective-permute-start(f32[80,128]{1,0:T(8,128)S(1)} %get-tuple-element.52.own), channel_id=1, source_target_pairs={{0,4},{4,0},{8,12},{12,8},{1,5},{5,1},{9,13},{13,9},{2,6},{6,2},{1... | collective-permute-start | bytes 122888 | tf_op jit(solution)/shard_map/ppermute | solution.py:35
  37.5 1.1 %collective-permute-start.9 = (f32[80,128]{1,0:T(8,128)S(1)}, f32[80,128]{1,0:T(8,128)S(1)}, u32[]{:S(2)}, u32[]{:S(2)}) collective-permute-start(f32[80,128]{1,0:T(8,128)S(1)} %get-tuple-element.52.own), channel_id=1, source_target_pairs={{0,8},{4,12},{8,0},{12,4},{1,9},{5,13},{9,1},{13,5},{2,10},{6,14},... | collective-permute-start | bytes 122888 | tf_op jit(solution)/shard_map/ppermute | solution.py:35
  38.6 1.4 %collective-permute-start.10 = (f32[80,128]{1,0:T(8,128)S(1)}, f32[80,128]{1,0:T(8,128)S(1)}, u32[]{:S(2)}, u32[]{:S(2)}) collective-permute-start(f32[80,128]{1,0:T(8,128)S(1)} %get-tuple-element.52.own), channel_id=1, source_target_pairs={{0,12},{4,8},{8,4},{12,0},{1,13},{5,9},{9,5},{13,1},{2,14},{6,10},... | collective-permute-start | bytes 122888 | tf_op jit(solution)/shard_map/ppermute | solution.py:35
  40.0 1.4 %shard_map.118 = (f32[4096,80]{1,0:T(8,128)S(1)}, bf16[80,4096]{1,0:T(8,128)(2,1)S(1)}) custom-call(bf16[80,12288]{1,0:T(8,128)(2,1)S(1)} %get-tuple-element.54.exps, bf16[40,4096]{1,0:T(8,128)(2,1)S(1)} %get-tuple-element.55.v0, bf16[40,4096]{1,0:T(8,128)(2,1)S(1)} %collective-permute-done.11.v1, bf16[256,4096]{1,0:T(8,128)(2,1)S(1)} %get-tuple-element.56.refv, ...), custom_call_target="tpu_custom_call" | custom-call | flops 220200960 | tf_op jit(solution)/shard_map/pallas_call | solution.py:337
  41.5 1.4 %shard_map.119.late = f32[4096,80]{1,0:T(8,128)S(1)} custom-call(bf16[40,9216]{1,0:T(8,128)(2,1)S(1)} %get-tuple-element.59.first, bf16[40,3072]{1,0:T(8,128)(2,1)S(1)} %get-tuple-element.60.second, bf16[40,12288]{1,0:T(8,128)(2,1)S(1)} %get-tuple-element.61.far, bf16[80,4096]{1,0:T(8,128)(2,1)S(1)} %get-tuple-element.62.values, ...), custom_call_target="tpu_custom_call" | custom-call | flops 220200960 | tf_op jit(solution)/shard_map/pallas_call | solution.py:337
  42.9 1.6 %collective-permute-done.10.o3 = f32[80,128]{1,0:T(8,128)S(1)} collective-permute-done((f32[80,128]{1,0:T(8,128)S(1)}, f32[80,128]{1,0:T(8,128)S(1)}, u32[]{:S(2)}, u32[]{:S(2)}) %collective-permute-start.10) | collective-permute-done | bytes 40992 | tf_op jit(solution)/shard_map/ppermute | solution.py:35
  44.5 0.7 %shard_map.120 = (f32[10,128]{1,0:T(8,128)S(1)}, f32[10,128]{1,0:T(8,128)S(1)}, f32[20,128]{1,0:T(8,128)S(1)}, f32[56,128]{1,0:T(8,128)S(1)}) custom-call(f32[24,128]{1,0:T(8,128)S(1)} %get-tuple-element.36.scalars, f32[80,128]{1,0:T(8,128)S(1)} %get-tuple-element.52.own, f32[80,128]{1,0:T(8,128)S(1)} %collective-permute-done.8.o1, ...), custom_call_target="tpu_custom_call" | custom-call | tf_op jit(solution)/shard_map/pallas_call | solution.py:337
  45.2 1.2 %collective-permute-done.12.taken = f32[56,128]{1,0:T(8,128)S(1)} collective-permute-done((f32[56,128]{1,0:T(8,128)S(1)}, f32[56,128]{1,0:T(8,128)S(1)}, u32[]{:S(2)}, u32[]{:S(2)}) %collective-permute-start.12) | collective-permute-done | bytes 28704 | tf_op jit(solution)/shard_map/ppermute | solution.py:35
  46.5 3.6 %collective-permute-done.14.side = f32[20,128]{1,0:T(8,128)S(1)} collective-permute-done((f32[20,128]{1,0:T(8,128)S(1)}, f32[20,128]{1,0:T(8,128)S(1)}, u32[]{:S(2)}, u32[]{:S(2)}) %collective-permute-start.14) | collective-permute-done | bytes 10272 | tf_op jit(solution)/shard_map/ppermute | solution.py:35
  50.1 0.8 %collective-permute-start.15 = (f32[20,128]{1,0:T(8,128)S(1)}, f32[20,128]{1,0:T(8,128)S(1)}, u32[]{:S(2)}, u32[]{:S(2)}) collective-permute-start(f32[20,128]{1,0:T(8,128)S(1)} %collective-permute-done.14.side), channel_id=1, source_target_pairs={{0,1},{1,0},{2,3},{3,2},{4,5},{5,4},{6,7},{7,6},{8,9},{9,8},{10,11... | collective-permute-start | bytes 30728 | tf_op jit(solution)/shard_map/ppermute | solution.py:35
  50.9 4.5 %collective-permute-done.13.across = f32[10,128]{1,0:T(8,128)S(1)} collective-permute-done((f32[10,128]{1,0:T(8,128)S(1)}, f32[10,128]{1,0:T(8,128)S(1)}, u32[]{:S(2)}, u32[]{:S(2)}) %collective-permute-start.13) | collective-permute-done | bytes 5152 | tf_op jit(solution)/shard_map/ppermute | solution.py:35
  (22 shorter events, 2.3 us)
Async XLA Ops:
  0.6 13.0 %collective-permute-start.1 = (bf16[40,4096]{1,0:T(8,128)(2,1)}, bf16[40,4096]{1,0:T(8,128)(2,1)S(1)}, u32[]{:S(2)}, u32[]{:S(2)}) collective-permute-start(bf16[40,4096]{1,0:T(8,128)(2,1)} %bitcast.8), channel_id=1, source_target_pairs={{4,8},{8,4},{5,9},{9,5},{6,10},{10,6},{7,11},{11,7},{20,24},{24,20... | collective-permute-start | bytes 983048 | tf_op jit(solution)/shard_map/ppermute | solution.py:35
  1.3 17.0 %collective-permute-start.3 = (bf16[40,4096]{1,0:T(8,128)(2,1)}, bf16[40,4096]{1,0:T(8,128)(2,1)S(1)}, u32[]{:S(2)}, u32[]{:S(2)}) collective-permute-start(bf16[40,4096]{1,0:T(8,128)(2,1)} %bitcast.9), channel_id=1, source_target_pairs={{0,4},{4,0},{8,12},{12,8},{1,5},{5,1},{9,13},{13,9},{2,6},{6,2},{1... | collective-permute-start | bytes 983048 | tf_op jit(solution)/shard_map/ppermute | solution.py:35
  7.2 12.4 %collective-permute-start.4 = (bf16[40,4096]{1,0:T(8,128)(2,1)}, bf16[40,4096]{1,0:T(8,128)(2,1)S(1)}, u32[]{:S(2)}, u32[]{:S(2)}) collective-permute-start(bf16[40,4096]{1,0:T(8,128)(2,1)} %bitcast.14), channel_id=1, source_target_pairs={{0,2},{2,0},{1,3},{3,1},{4,6},{6,4},{5,7},{7,5},{8,10},{10,8},{9,1... | collective-permute-start | bytes 983048 | tf_op jit(solution)/shard_map/ppermute | solution.py:35
  8.7 15.6 %collective-permute-start.5 = (bf16[40,4096]{1,0:T(8,128)(2,1)}, bf16[40,4096]{1,0:T(8,128)(2,1)S(1)}, u32[]{:S(2)}, u32[]{:S(2)}) collective-permute-start(bf16[40,4096]{1,0:T(8,128)(2,1)} %bitcast.10), channel_id=1, source_target_pairs={{0,12},{12,0},{1,13},{13,1},{2,14},{14,2},{3,15},{15,3},{16,28},{2... | collective-permute-start | bytes 983048 | tf_op jit(solution)/shard_map/ppermute | solution.py:35
  12.0 28.0 %collective-permute-start.11 = (bf16[40,4096]{1,0:T(8,128)(2,1)}, bf16[40,4096]{1,0:T(8,128)(2,1)S(1)}, u32[]{:S(2)}, u32[]{:S(2)}) collective-permute-start(bf16[40,4096]{1,0:T(8,128)(2,1)} %bitcast.16), channel_id=1, source_target_pairs={{0,2},{2,0},{1,3},{3,1},{4,6},{6,4},{5,7},{7,5},{8,10},{10,8},{9,1... | collective-permute-start | bytes 983048 | tf_op jit(solution)/shard_map/ppermute | solution.py:35
  13.6 19.7 %collective-permute-start.6 = (bf16[40,3072]{1,0:T(8,128)(2,1)S(1)}, bf16[40,3072]{1,0:T(8,128)(2,1)S(1)}, u32[]{:S(2)}, u32[]{:S(2)}) collective-permute-start(bf16[40,3072]{1,0:T(8,128)(2,1)S(1)} %get-tuple-element.48), channel_id=1, source_target_pairs={{0,8},{12,4},{1,9},{13,5},{2,10},{14,6},{3,11},{15,7},{16,24},{28,... | collective-permute-start | bytes 737288 | tf_op jit(solution)/shard_map/ppermute | solution.py:35
  18.3 15.0 %collective-permute-start.7 = (bf16[40,3072]{1,0:T(8,128)(2,1)S(1)}, bf16[40,3072]{1,0:T(8,128)(2,1)S(1)}, u32[]{:S(2)}, u32[]{:S(2)}) collective-permute-start(bf16[40,3072]{1,0:T(8,128)(2,1)S(1)} %get-tuple-element.49), channel_id=1, source_target_pairs={{8,12},{4,0},{9,13},{5,1},{10,14},{6,2},{11,15},{7,3},{24,28},{20,... | collective-permute-start | bytes 737288 | tf_op jit(solution)/shard_map/ppermute | solution.py:35
  19.7 14.6 %collective-permute-start = (bf16[40,1024]{1,0:T(8,128)(2,1)S(1)}, bf16[40,1024]{1,0:T(8,128)(2,1)S(1)}, u32[]{:S(2)}, u32[]{:S(2)}) collective-permute-start(bf16[40,1024]{1,0:T(8,128)(2,1)S(1)} %get-tuple-element.37), channel_id=1, source_target_pairs={{0,8},{12,4},{1,9},{13,5},{2,10},{14,6},{3,11},{15,7},{16,24},{28,... | collective-permute-start | bytes 245768 | tf_op jit(solution)/shard_map/ppermute | solution.py:35
  24.4 9.9 %collective-permute-start.2 = (bf16[40,1024]{1,0:T(8,128)(2,1)S(1)}, bf16[40,1024]{1,0:T(8,128)(2,1)S(1)}, u32[]{:S(2)}, u32[]{:S(2)}) collective-permute-start(bf16[40,1024]{1,0:T(8,128)(2,1)S(1)} %get-tuple-element.38), channel_id=1, source_target_pairs={{8,12},{4,0},{9,13},{5,1},{10,14},{6,2},{11,15},{7,3},{24,28},{20,... | collective-permute-start | bytes 245768 | tf_op jit(solution)/shard_map/ppermute | solution.py:35
  34.8 8.0 %collective-permute-start.8 = (f32[80,128]{1,0:T(8,128)S(1)}, f32[80,128]{1,0:T(8,128)S(1)}, u32[]{:S(2)}, u32[]{:S(2)}) collective-permute-start(f32[80,128]{1,0:T(8,128)S(1)} %get-tuple-element.52.own), channel_id=1, source_target_pairs={{0,4},{4,0},{8,12},{12,8},{1,5},{5,1},{9,13},{13,9},{2,6},{6,2},{1... | collective-permute-start | bytes 122888 | tf_op jit(solution)/shard_map/ppermute | solution.py:35
  37.5 5.3 %collective-permute-start.9 = (f32[80,128]{1,0:T(8,128)S(1)}, f32[80,128]{1,0:T(8,128)S(1)}, u32[]{:S(2)}, u32[]{:S(2)}) collective-permute-start(f32[80,128]{1,0:T(8,128)S(1)} %get-tuple-element.52.own), channel_id=1, source_target_pairs={{0,8},{4,12},{8,0},{12,4},{1,9},{5,13},{9,1},{13,5},{2,10},{6,14},... | collective-permute-start | bytes 122888 | tf_op jit(solution)/shard_map/ppermute | solution.py:35
  38.6 5.8 %collective-permute-start.10 = (f32[80,128]{1,0:T(8,128)S(1)}, f32[80,128]{1,0:T(8,128)S(1)}, u32[]{:S(2)}, u32[]{:S(2)}) collective-permute-start(f32[80,128]{1,0:T(8,128)S(1)} %get-tuple-element.52.own), channel_id=1, source_target_pairs={{0,12},{4,8},{8,4},{12,0},{1,13},{5,9},{9,5},{13,1},{2,14},{6,10},... | collective-permute-start | bytes 122888 | tf_op jit(solution)/shard_map/ppermute | solution.py:35
  44.5 11.0 %copy-start = (f32[10,128]{1,0:T(8,128)S(1)}, f32[10,128]{1,0:T(8,128)}, u32[]{:S(2)}) copy-start(f32[10,128]{1,0:T(8,128)} %latent.1) | copy-start | bytes 15364
  45.1 1.3 %collective-permute-start.12 = (f32[56,128]{1,0:T(8,128)S(1)}, f32[56,128]{1,0:T(8,128)S(1)}, u32[]{:S(2)}, u32[]{:S(2)}) collective-permute-start(f32[56,128]{1,0:T(8,128)S(1)} %get-tuple-element.63), channel_id=1, source_target_pairs={{0,1},{1,0},{2,3},{3,2},{4,5},{5,4},{6,7},{7,6},{8,9},{9,8},{10,11... | collective-permute-start | bytes 86024 | tf_op jit(solution)/shard_map/ppermute | solution.py:35
  46.4 3.7 %collective-permute-start.14 = (f32[20,128]{1,0:T(8,128)S(1)}, f32[20,128]{1,0:T(8,128)S(1)}, u32[]{:S(2)}, u32[]{:S(2)}) collective-permute-start(f32[20,128]{1,0:T(8,128)S(1)} %get-tuple-element.69), channel_id=1, source_target_pairs={{0,4},{4,0},{8,12},{12,8},{1,13},{5,9},{9,5},{13,1},{2,6},{6,2},{1... | collective-permute-start | bytes 30728 | tf_op jit(solution)/shard_map/ppermute | solution.py:35
  50.1 5.4 %collective-permute-start.15 = (f32[20,128]{1,0:T(8,128)S(1)}, f32[20,128]{1,0:T(8,128)S(1)}, u32[]{:S(2)}, u32[]{:S(2)}) collective-permute-start(f32[20,128]{1,0:T(8,128)S(1)} %collective-permute-done.14.side), channel_id=1, source_target_pairs={{0,1},{1,0},{2,3},{3,2},{4,5},{5,4},{6,7},{7,6},{8,9},{9,8},{10,11... | collective-permute-start | bytes 30728 | tf_op jit(solution)/shard_map/ppermute | solution.py:35
  50.9 4.5 %collective-permute-start.13 = (f32[10,128]{1,0:T(8,128)S(1)}, f32[10,128]{1,0:T(8,128)S(1)}, u32[]{:S(2)}, u32[]{:S(2)}) collective-permute-start(f32[10,128]{1,0:T(8,128)S(1)} %get-tuple-element.68), channel_id=1, source_target_pairs={{0,8},{4,12},{8,0},{12,4},{1,9},{5,13},{9,1},{13,5},{2,10},{6,14},... | collective-permute-start | bytes 15368 | tf_op jit(solution)/shard_map/ppermute | solution.py:35
